TPU v7x, 16 devices: a 4x2x1 block of a 4x4x8 slice. The times are simulated.
16 devices in a mesh: dp: 2 (over y, z), tp: 8 (over x, core).
Axes of the slice: x: 4, y: 2, z: 1, core: 2. Of those that a mesh axis runs over, the one named last changes fastest.
The devices are a block of a 4x4x8 slice.
Arguments:
- hidden: bfloat16 [4, 2048, 512], P('dp', 'tp'), parts along dimension 0
- grad_out: bfloat16 [4, 2048, 512], P('dp', 'tp'), parts along dimension 0
- ln1_gain: bfloat16 [512], replicated
- ln1_bias: bfloat16 [512], replicated
- w_qkv: bfloat16 [512, 3, 8, 64], P(None, None, 'tp')
- b_qkv: bfloat16 [3, 8, 64], P(None, 'tp')
- w_out: bfloat16 [8, 64, 512], P('tp')
- b_out: bfloat16 [512], replicated
- ln2_gain: bfloat16 [512], replicated
- ln2_bias: bfloat16 [512], replicated
- w_up: bfloat16 [512, 2048], P(None, 'tp')
- b_up: bfloat16 [2048], P('tp')
- w_down: bfloat16 [2048, 512], P('tp')
- b_down: bfloat16 [512], replicated
Outputs:
- output 1: bfloat16 [4, 2048, 512], P('dp', 'tp'), parts along dimension 0
- output 2: bfloat16 [4, 2048, 512], P('dp', 'tp'), parts along dimension 0
- output 3: float32 [1024], P('dp'), parts along dimension 0
- output 4: float32 [1024], P('dp'), parts along dimension 0
- output 5: float32 [1024, 3, 8, 64], P('dp', None, 'tp'), parts along dimension 0
- output 6: float32 [6, 8, 64], P('dp', 'tp'), parts along dimension 0
- output 7: float32 [16, 64, 512], P(('dp', 'tp')), parts along dimension 0
- output 8: float32 [1024], P('dp'), parts along dimension 0
- output 9: float32 [1024], P('dp'), parts along dimension 0
- output 10: float32 [1024], P('dp'), parts along dimension 0
- output 11: float32 [1024, 2048], P('dp', 'tp'), parts along dimension 0
- output 12: float32 [4096], P(('dp', 'tp')), parts along dimension 0
- output 13: float32 [4096, 512], P(('dp', 'tp')), parts along dimension 0
- output 14: float32 [1024], P('dp'), parts along dimension 0
There are 2 independent parts. A program takes and returns all parts, laid end to end along the dimension named above; an argument that names none is the same for every part.
All inputs are finite; a program needn't handle non-finite values.
Results may differ from a plain program's by a relative error of at most 0.0187336.
Values are sent between devices in bfloat16 or wider.
A program may use at most 768 MiB of HBM per device.

v0:
```python
import jax
import jax.numpy as jnp
from jax import lax
from jax.sharding import PartitionSpec as P

LN_EPS = 1e-5


def norm_forward(value, gain, shift):
    val32 = value.astype(jnp.float32)
    centered = val32 - jnp.mean(val32, axis=-1, keepdims=True)
    inv_std = lax.rsqrt(jnp.mean(centered * centered, axis=-1, keepdims=True) + LN_EPS)
    x_hat = centered * inv_std
    normed = x_hat * gain.astype(jnp.float32) + shift.astype(jnp.float32)
    return normed.astype(jnp.bfloat16), x_hat, inv_std


def norm_backward(grad_normed, x_hat, inv_std, gain):
    grad32 = grad_normed.astype(jnp.float32)
    grad_gain = jnp.sum(grad32 * x_hat, axis=(0, 1))
    grad_shift = jnp.sum(grad32, axis=(0, 1))
    value_a9 = grad32 * gain.astype(jnp.float32)
    grad_input = inv_std * (value_a9 - jnp.mean(value_a9, axis=-1, keepdims=True) - x_hat * jnp.mean(value_a9 * x_hat, axis=-1, keepdims=True))
    return grad_input, grad_gain, grad_shift


def gelu_tanh(value):
    return jax.nn.gelu(value, approximate=True)


def attention_forward(qkv_proj, attn_scale):
    seq_len = qkv_proj.shape[2]
    scores = jnp.einsum("bqhe,bkhe->bhqk", qkv_proj[0], qkv_proj[1], preferred_element_type=jnp.float32) * attn_scale
    positions = jnp.arange(seq_len)
    causal = positions[:, None] >= positions[None, :]
    probs32 = jax.nn.softmax(jnp.where(causal, scores, -1e30), axis=-1)
    probs_bf = probs32.astype(jnp.bfloat16)
    context = jnp.einsum("bhqk,bkhe->bqhe", probs_bf, qkv_proj[2], preferred_element_type=jnp.float32).astype(jnp.bfloat16)
    return context, probs32, probs_bf


def attention_backward(grad_context, qkv_proj, probs32, probs_bf, attn_scale):
    grad_probs = jnp.einsum("bqhe,bkhe->bhqk", grad_context, qkv_proj[2], preferred_element_type=jnp.float32).astype(jnp.bfloat16).astype(jnp.float32)
    row_dot = jnp.sum(grad_probs * probs32, axis=-1, keepdims=True)
    grad_scores = (probs32 * (grad_probs - row_dot) * attn_scale).astype(jnp.bfloat16)
    grad_query = jnp.einsum("bhqk,bkhe->bqhe", grad_scores, qkv_proj[1], preferred_element_type=jnp.float32)
    grad_key = jnp.einsum("bhqk,bqhe->bkhe", grad_scores, qkv_proj[0], preferred_element_type=jnp.float32)
    grad_value = jnp.einsum("bhqk,bqhe->bkhe", probs_bf, grad_context, preferred_element_type=jnp.float32)
    return jnp.stack([grad_query.astype(jnp.bfloat16), grad_key.astype(jnp.bfloat16), grad_value.astype(jnp.bfloat16)])


def solution(mesh):
    def device_step(hidden, grad_out, ln1_gain, ln1_bias, w_qkv, b_qkv, w_out, b_out, ln2_gain, ln2_bias, w_up, b_up, w_down, b_down):
        attn_scale = w_qkv.shape[-1] ** -0.5
        normed1, x_hat1, inv_std1 = norm_forward(hidden, ln1_gain, ln1_bias)
        normed1_all = lax.all_gather(normed1, "tp", axis=1, tiled=True)
        qkv_proj = (jnp.einsum("bsd,dche->cbshe", normed1_all, w_qkv, preferred_element_type=jnp.float32) + b_qkv.astype(jnp.float32)[:, None, None]).astype(jnp.bfloat16)
        context, probs32, probs_bf = attention_forward(qkv_proj, attn_scale)
        attn_part = jnp.einsum("crif,ife->cre", context, w_out, preferred_element_type=jnp.float32).astype(jnp.bfloat16)
        attn_local = lax.psum_scatter(attn_part, "tp", scatter_dimension=1, tiled=True)
        resid1 = (hidden.astype(jnp.float32) + attn_local.astype(jnp.float32) + b_out.astype(jnp.float32)).astype(jnp.bfloat16)
        normed2, x_hat2, inv_std2 = norm_forward(resid1, ln2_gain, ln2_bias)
        normed2_all = lax.all_gather(normed2, "tp", axis=1, tiled=True)
        pre_act = (jnp.einsum("bsd,df->bsf", normed2_all, w_up, preferred_element_type=jnp.float32) + b_up.astype(jnp.float32)).astype(jnp.bfloat16)
        gelu_val, gelu_pull = jax.vjp(gelu_tanh, pre_act.astype(jnp.float32))
        gelu_out = gelu_val.astype(jnp.bfloat16)
        mlp_part = jnp.einsum("bsf,fd->bsd", gelu_out, w_down, preferred_element_type=jnp.float32).astype(jnp.bfloat16)
        mlp_local = lax.psum_scatter(mlp_part, "tp", scatter_dimension=1, tiled=True)
        layer_out = (resid1.astype(jnp.float32) + mlp_local.astype(jnp.float32) + b_down.astype(jnp.float32)).astype(jnp.bfloat16)

        grad_out_all = lax.all_gather(grad_out, "tp", axis=1, tiled=True)
        grad_b_down = jnp.sum(grad_out, axis=(0, 1), dtype=jnp.float32)
        grad_gelu = jnp.einsum("bsd,fd->bsf", grad_out_all, w_down, preferred_element_type=jnp.float32).astype(jnp.bfloat16)
        grad_w_down = jnp.einsum("bsf,bsd->fd", gelu_out, grad_out_all, preferred_element_type=jnp.float32)
        grad_pre = gelu_pull(grad_gelu.astype(jnp.float32))[0].astype(jnp.bfloat16)
        grad_b_up = jnp.sum(grad_pre, axis=(0, 1), dtype=jnp.float32)
        grad_w_up = jnp.einsum("bsd,bsf->df", normed2_all, grad_pre, preferred_element_type=jnp.float32)
        grad_norm2_part = jnp.einsum("bsf,df->bsd", grad_pre, w_up, preferred_element_type=jnp.float32).astype(jnp.bfloat16)
        grad_norm2 = lax.psum_scatter(grad_norm2_part, "tp", scatter_dimension=1, tiled=True)
        grad_resid_ln, grad_ln2_gain, grad_ln2_bias = norm_backward(grad_norm2, x_hat2, inv_std2, ln2_gain)
        grad_resid1 = (grad_out.astype(jnp.float32) + grad_resid_ln).astype(jnp.bfloat16)
        grad_b_out = jnp.sum(grad_resid1, axis=(0, 1), dtype=jnp.float32)
        grad_resid1_all = lax.all_gather(grad_resid1, "tp", axis=1, tiled=True)
        grad_context = jnp.einsum("cre,ife->crif", grad_resid1_all, w_out, preferred_element_type=jnp.float32).astype(jnp.bfloat16)
        grad_w_out = jnp.einsum("crif,cre->ife", context, grad_resid1_all, preferred_element_type=jnp.float32)
        grad_qkv = attention_backward(grad_context, qkv_proj, probs32, probs_bf, attn_scale)
        grad_b_qkv = jnp.sum(grad_qkv, axis=(1, 2), dtype=jnp.float32)
        grad_w_qkv = jnp.einsum("bsd,cbshe->dche", normed1_all, grad_qkv, preferred_element_type=jnp.float32)
        grad_norm1_part = jnp.einsum("cbshe,dche->bsd", grad_qkv, w_qkv, preferred_element_type=jnp.float32).astype(jnp.bfloat16)
        grad_norm1 = lax.psum_scatter(grad_norm1_part, "tp", scatter_dimension=1, tiled=True)
        grad_input_ln, grad_ln1_gain, grad_ln1_bias = norm_backward(grad_norm1, x_hat1, inv_std1, ln1_gain)
        grad_hidden = (grad_resid1.astype(jnp.float32) + grad_input_ln).astype(jnp.bfloat16)
        vec_sums = lax.psum(jnp.stack([grad_ln1_gain, grad_ln1_bias, grad_b_out, grad_ln2_gain, grad_ln2_bias, grad_b_down]), "tp")
        return (layer_out, grad_hidden, vec_sums[0], vec_sums[1], grad_w_qkv, grad_b_qkv, grad_w_out, vec_sums[2], vec_sums[3], vec_sums[4], grad_w_up, grad_b_up, grad_w_down, vec_sums[5])

    act_spec = P("dp", "tp", None)
    vec_spec = P(None)
    group_vec = P("dp")
    in_specs = (act_spec, act_spec, vec_spec, vec_spec, P(None, None, "tp", None), P(None, "tp", None), P("tp", None, None), vec_spec, vec_spec, vec_spec, P(None, "tp"), P("tp"), P("tp", None), vec_spec)
    out_specs = (act_spec, act_spec, group_vec, group_vec, P("dp", None, "tp", None), P("dp", "tp", None), P(("dp", "tp"), None, None), group_vec, group_vec, group_vec, P("dp", "tp"), P(("dp", "tp")), P(("dp", "tp"), None), group_vec)
    return jax.shard_map(device_step, mesh=mesh, in_specs=in_specs, out_specs=out_specs, check_vma=False)
```

profile of v0, /device:TPU:112, one launch (start us, length us, event | category | flops | bytes accessed | tf_op | source)
XLA Modules:
  0.0 453.7 jit_solution(17405296852200223998)
XLA Ops:
  11.9 2.1 fusion.82
  14.8 4.2 iota_compare_fusion
  18.9 25.8 %all-gather.5.cloned.1.call-done = bf16[2,2048,512]{2,1,0:T(8,128)(2,1)} async-done(((bf16[2,256,512]{2,1,0:T(8,128)(2,1)}), bf16[2,2048,512]{2,1,0:T(8,128)(2,1)}) %all-gather.5.cloned.1.call-update) | async-done | bytes 4194320 | tf_op jit(solution)/shard_map/all_gather | solution.py:56
  44.8 3.7 fusion.36
  48.5 19.2 %fusion.116 = (f32[2,2048]{1,0:T(2,128)S(1)}, f32[2,2048,2048]{1,2,0:T(8,128)}) fusion(pred[2048,2048]{0,1:T(8,128)(4,1)} %iota_compare_fusion, bf16[3,2,2048,1,64]{2,4,0,1,3:T(8,128)(2,1)S(1)} %fusion.36), kind=kOutput, calls=%fused_computation.150 | convolution fusion | flops 1107298304 | bytes 38813696 | tf_op jit(solution)/shard_map/sub | solution.py:36
  67.8 12.2 %fusion.52 = bf16[2,2048,64]{1,2,0:T(8,128)(2,1)S(1)} fusion(bf16[3,2,2048,1,64]{2,4,0,1,3:T(8,128)(2,1)S(1)} %fusion.36, f32[2,2048,2048]{1,2,0:T(8,128)} %get-tuple-element.49, f32[2,2048]{1,0:T(2,128)S(1)} %get-tuple-element.48), kind=kOutput, calls=%fused_computation.64 | convolution fusion | flops 1090781184 | bytes 34619392 | tf_op jit(solution)/shard_map/bhqk,bkhe->bqhe/dot_general | solution.py:38
  80.9 3.3 convolution_convert_fusion.3
  84.4 33.8 %reduce-scatter.5.cloned.1.call-done = bf16[2,256,512]{2,1,0:T(8,128)(2,1)} async-done(((bf16[2,2048,512]{2,1,0:T(8,128)(2,1)}), bf16[2,256,512]{2,1,0:T(8,128)(2,1)}) %reduce-scatter.5.cloned.1.call-update) | async-done | bytes 524304 | tf_op jit(solution)/shard_map/reduce_scatter | solution.py:60
  122.0 25.8 %all-gather.7.cloned.1.call-done = bf16[2,2048,512]{2,1,0:T(8,128)(2,1)} async-done(((bf16[2,256,512]{2,1,0:T(8,128)(2,1)}), bf16[2,2048,512]{2,1,0:T(8,128)(2,1)}) %all-gather.7.cloned.1.call-update) | async-done | bytes 4194320 | tf_op jit(solution)/shard_map/all_gather | solution.py:63
  147.7 4.8 %add_convert_fusion = bf16[2,2048,256]{2,1,0:T(8,128)(2,1)} fusion(bf16[2,2048,512]{2,1,0:T(8,128)(2,1)} %all-gather.7.cloned.1.call-done, f32[256]{0:T(256)S(1)} %convert_element_type.194, bf16[512,256]{1,0:T(8,128)(2,1)S(1)} %copy-done.12), kind=kOutput, calls=%fused_computation.46 | convolution fusion | flops 1075838976 | bytes 6554624 | tf_op jit(solution)/shard_map/bsd,df->bsf/dot_general | solution.py:64
  152.5 24.3 %all-gather.9.cloned.1.call-done = bf16[2,2048,512]{2,1,0:T(8,128)(2,1)} async-done(((bf16[2,256,512]{2,1,0:T(8,128)(2,1)}), bf16[2,2048,512]{2,1,0:T(8,128)(2,1)}) %all-gather.9.cloned.1.call-update) | async-done | bytes 4194320 | tf_op jit(solution)/shard_map/all_gather | solution.py:71
  176.9 6.7 %convert_reduce_fusion = (f32[256]{0:T(256)}, bf16[2,2048,256]{2,1,0:T(8,128)(2,1)S(1)}) fusion(bf16[2,2048,256]{2,1,0:T(8,128)(2,1)} %add_convert_fusion, bf16[2,2048,512]{2,1,0:T(8,128)(2,1)} %all-gather.9.cloned.1.call-done, bf16[256,512]{1,0:T(8,128)(2,1)S(1)} %copy-done), kind=kOutput, calls=%fused_computation.45 | convolution fusion | flops 1099955968 | bytes 8651776 | tf_op jit(solution)/shard_map/bsd,fd->bsf/dot_general | solution.py:73
  183.6 3.3 convolution_convert_fusion.1
  187.0 5.3 %convolution_convert_fusion.2 = bf16[2,2048,512]{2,1,0:T(8,128)(2,1)} fusion(bf16[256,512]{1,0:T(8,128)(2,1)S(1)} %copy-done, bf16[2,2048,256]{2,1,0:T(8,128)(2,1)} %add_convert_fusion), kind=kOutput, calls=%fused_computation.49 | convolution fusion | flops 1086324736 | bytes 6553600 | tf_op jit(solution)/shard_map/bsf,fd->bsd/dot_general | solution.py:67
  193.0 28.0 %reduce-scatter.9.cloned.1.call-done = bf16[2,256,512]{2,1,0:T(8,128)(2,1)} async-done(((bf16[2,2048,512]{2,1,0:T(8,128)(2,1)}), bf16[2,256,512]{2,1,0:T(8,128)(2,1)}) %reduce-scatter.9.cloned.1.call-update) | async-done | bytes 524304 | tf_op jit(solution)/shard_map/reduce_scatter | solution.py:79
  221.0 1.6 fusion.94
  222.6 33.2 %reduce-scatter.7.cloned.1.call-done = bf16[2,256,512]{2,1,0:T(8,128)(2,1)} async-done(((bf16[2,2048,512]{2,1,0:T(8,128)(2,1)}), bf16[2,256,512]{2,1,0:T(8,128)(2,1)}) %reduce-scatter.7.cloned.1.call-update) | async-done | bytes 524304 | tf_op jit(solution)/shard_map/reduce_scatter | solution.py:68
  255.9 2.8 convert_reduce_fusion.6
  259.3 26.1 %all-gather.11.cloned.1.call-done = bf16[2,2048,512]{2,1,0:T(8,128)(2,1)} async-done(((bf16[2,256,512]{2,1,0:T(8,128)(2,1)}), bf16[2,2048,512]{2,1,0:T(8,128)(2,1)}) %all-gather.11.cloned.1.call-update) | async-done | bytes 4194320 | tf_op jit(solution)/shard_map/all_gather | solution.py:83
  285.4 3.6 convolution_convert_fusion.5
  289.0 13.3 %fusion.49 = bf16[1,2,2048,1,64]{2,4,1,3,0:T(8,128)(2,1)S(1)} fusion(bf16[2,2048,64]{1,2,0:T(8,128)(2,1)S(1)} %convolution_convert_fusion.5, f32[2,2048,2048]{1,2,0:T(8,128)} %get-tuple-element.49, f32[2,2048]{1,0:T(2,128)S(1)} %get-tuple-element.48), kind=kOutput, calls=%fused_computation.63 | convolution fusion | flops 1090781184 | bytes 34619392 | tf_op jit(solution)/shard_map/bhqk,bqhe->bkhe/dot_general | solution.py:48
  302.3 9.2 %convolution_convert_fusion = bf16[2,2048,2048]{1,2,0:T(8,128)(2,1)} fusion(bf16[2,2048,64]{1,2,0:T(8,128)(2,1)S(1)} %convolution_convert_fusion.5, bf16[3,2,2048,1,64]{2,4,0,1,3:T(8,128)(2,1)} %copy-done.14), kind=kOutput, calls=%fused_computation.16 | convolution fusion | flops 1082130432 | bytes 17825792 | tf_op jit(solution)/shard_map/bqhe,bkhe->bhqk/dot_general | solution.py:43
  311.5 33.4 %fusion.48 = bf16[1,2,2048,1,64]{2,4,1,3,0:T(8,128)(2,1)S(1)} fusion(bf16[2,2048,2048]{1,2,0:T(8,128)(2,1)} %convolution_convert_fusion, bf16[3,2,2048,1,64]{2,4,0,1,3:T(8,128)(2,1)} %copy-done.14, f32[2,2048,2048]{1,2,0:T(8,128)} %get-tuple-element.49, f32[2,2048]{1,0:T(2,128)S(1)} %get-tuple-element.48), kind=kOutput, calls=%fused_computation.62 | convolution fusion | flops 1149507584 | bytes 101744640 | tf_op jit(solution)/shard_map/bhqk,bkhe->bqhe/dot_general | solution.py:46
  344.9 34.7 %fusion.47 = bf16[1,2,2048,1,64]{2,4,1,3,0:T(8,128)(2,1)} fusion(bf16[2,2048,2048]{1,2,0:T(8,128)(2,1)} %convolution_convert_fusion, bf16[3,2,2048,1,64]{2,4,0,1,3:T(8,128)(2,1)} %copy-done.14, f32[2,2048,2048]{1,2,0:T(8,128)} %get-tuple-element.49, f32[2,2048]{1,0:T(2,128)S(1)} %get-tuple-element.48), kind=kOutput, calls=%fused_computation.61 | convolution fusion | flops 1149507584 | bytes 101744640 | tf_op jit(solution)/shard_map/bhqk,bqhe->bkhe/dot_general | solution.py:47
  379.6 4.3 bitcast_convert_fusion
  384.0 4.4 convolution_bitcast_fusion.1
  388.4 2.7 convolution_bitcast_fusion
  393.6 1.7 fusion.71
  395.3 22.7 %reduce-scatter.11.cloned.1.call-done = bf16[2,256,512]{2,1,0:T(8,128)(2,1)} async-done(((bf16[2,2048,512]{2,1,0:T(8,128)(2,1)}), bf16[2,256,512]{2,1,0:T(8,128)(2,1)}) %reduce-scatter.11.cloned.1.call-update) | async-done | bytes 524304 | tf_op jit(solution)/shard_map/reduce_scatter | solution.py:90
  418.0 1.6 fusion.95
  419.7 24.0 %psum.7 = f32[6,512]{1,0:T(8,128)S(1)} all-reduce(f32[6,512]{1,0:T(8,128)S(1)} %stack.43), channel_id=1, replica_groups=mesh['dp'=2,'tp'=8] {'tp'}, use_global_device_ids=true, to_apply=%region_21.22 | all-reduce | flops 3072 | bytes 24576 | tf_op jit(solution)/shard_map/psum | solution.py:93
  444.3 2.3 fusion.87
  (103 shorter events, 14.6 us)
Async XLA Ops:
  7.2 169.7 %copy-start = (bf16[256,512]{1,0:T(8,128)(2,1)S(1)}, bf16[256,512]{1,0:T(8,128)(2,1)}, u32[]{:S(2)}) copy-start(bf16[256,512]{1,0:T(8,128)(2,1)} %param.26) | copy-start | bytes 786436
  7.2 37.6 %copy-start.27 = (bf16[512,3,1,64]{0,3,2,1:T(8,128)(2,1)S(1)}, bf16[512,3,1,64]{0,3,2,1:T(8,128)(2,1)}, u32[]{:S(2)}) copy-start(bf16[512,3,1,64]{0,3,2,1:T(8,128)(2,1)} %param.18) | copy-start | bytes 589828
  7.2 37.6 %all-gather.5.cloned.1.call-start = ((), (), s32[]{:S(2)}) async-start(), calls=%async_computation.4 | async-start | bytes 4718592 | tf_op jit(solution)/shard_map/all_gather | solution.py:56
  8.0 3.2 copy-start.17
  14.0 104.2 %reduce-scatter.5.cloned.1.call-start = ((), (), s32[]{:S(2)}) async-start(), calls=%async_computation.5 | async-start | bytes 4718592 | tf_op jit(solution)/shard_map/reduce_scatter | solution.py:60
  48.5 19.3 %copy-start.14 = (bf16[3,2,2048,1,64]{2,4,0,1,3:T(8,128)(2,1)}, bf16[3,2,2048,1,64]{2,4,0,1,3:T(8,128)(2,1)S(1)}, u32[]{:S(2)}) copy-start(bf16[3,2,2048,1,64]{2,4,0,1,3:T(8,128)(2,1)S(1)} %fusion.36) | copy-start | bytes 4718596
  67.8 13.1 %copy-start.13 = (bf16[1,64,512]{2,1,0:T(8,128)(2,1)S(1)}, bf16[1,64,512]{2,1,0:T(8,128)(2,1)}, u32[]{:S(2)}) copy-start(bf16[1,64,512]{2,1,0:T(8,128)(2,1)} %param.20) | copy-start | bytes 196612
  80.9 3.5 copy-start.21
  80.9 3.5 copy-start.22
  80.9 3.5 copy-start.23
  80.9 37.4 %copy-start.2 = (bf16[2,256,512]{2,1,0:T(8,128)(2,1)S(1)}, bf16[2,256,512]{2,1,0:T(8,128)(2,1)}, u32[]{:S(2)}) copy-start(bf16[2,256,512]{2,1,0:T(8,128)(2,1)} %param.14) | copy-start | bytes 1572868
  84.2 37.7 %copy-start.29 = (bf16[256]{0:T(256)(128)(2,1)S(1)}, bf16[256]{0:T(256)(128)(2,1)}, u32[]{:S(2)}) copy-start(bf16[256]{0:T(256)(128)(2,1)} %param.25) | copy-start | bytes 1540
  84.2 63.5 %copy-start.12 = (bf16[512,256]{1,0:T(8,128)(2,1)S(1)}, bf16[512,256]{1,0:T(8,128)(2,1)}, u32[]{:S(2)}) copy-start(bf16[512,256]{1,0:T(8,128)(2,1)} %param.24) | copy-start | bytes 786436
  84.3 63.5 %all-gather.7.cloned.1.call-start = ((), (), s32[]{:S(2)}) async-start(), calls=%async_computation.6 | async-start | bytes 4718592 | tf_op jit(solution)/shard_map/all_gather | solution.py:63
  121.0 55.9 %all-gather.9.cloned.1.call-start = ((), (), s32[]{:S(2)}) async-start(), calls=%async_computation.8 | async-start | bytes 4718592 | tf_op jit(solution)/shard_map/all_gather | solution.py:71
  121.6 99.4 %reduce-scatter.9.cloned.1.call-start = ((), (), s32[]{:S(2)}) async-start(), calls=%async_computation.9 | async-start | bytes 4718592 | tf_op jit(solution)/shard_map/reduce_scatter | solution.py:79
  187.0 68.9 %reduce-scatter.7.cloned.1.call-start = ((), (), s32[]{:S(2)}) async-start(), calls=%async_computation.7 | async-start | bytes 4718592 | tf_op jit(solution)/shard_map/reduce_scatter | solution.py:68
  192.3 63.5 %copy-start.8 = (bf16[2,256,512]{2,1,0:T(8,128)(2,1)S(1)}, bf16[2,256,512]{2,1,0:T(8,128)(2,1)}, u32[]{:S(2)}) copy-start(bf16[2,256,512]{2,1,0:T(8,128)(2,1)} %param.15) | copy-start | bytes 1572868
  192.4 93.1 %all-gather.11.cloned.1.call-start = ((), (), s32[]{:S(2)}) async-start(), calls=%async_computation.10 | async-start | bytes 4718592 | tf_op jit(solution)/shard_map/all_gather | solution.py:83
  258.8 159.2 %reduce-scatter.11.cloned.1.call-start = ((), (), s32[]{:S(2)}) async-start(), calls=%async_computation.11 | async-start | bytes 4718592 | tf_op jit(solution)/shard_map/reduce_scatter | solution.py:90
  344.9 46.3 %copy-start.9 = (bf16[1,2,2048,1,64]{2,4,1,3,0:T(8,128)(2,1)}, bf16[1,2,2048,1,64]{2,4,1,3,0:T(8,128)(2,1)S(1)}, u32[]{:S(2)}) copy-start(bf16[1,2,2048,1,64]{2,4,1,3,0:T(8,128)(2,1)S(1)} %fusion.48) | copy-start | bytes 1572868
  344.9 34.7 %copy-start.28 = (bf16[512,3,1,64]{0,3,2,1:T(8,128)(2,1)S(1)}, bf16[512,3,1,64]{0,3,2,1:T(8,128)(2,1)}, u32[]{:S(2)}) copy-start(bf16[512,3,1,64]{0,3,2,1:T(8,128)(2,1)} %param.18) | copy-start | bytes 589828
  384.0 4.4 copy-start.26
  384.0 4.4 copy-start.30
  388.4 3.6 copy-start.4
  388.4 3.6 copy-start.7
  393.5 24.4 %copy-start.3 = (bf16[2,256,512]{2,1,0:T(8,128)(2,1)S(1)}, bf16[2,256,512]{2,1,0:T(8,128)(2,1)}, u32[]{:S(2)}) copy-start(bf16[2,256,512]{2,1,0:T(8,128)(2,1)} %param.14) | copy-start | bytes 1572868
  393.5 24.4 %copy-start.16 = (f32[2,256]{1,0:T(2,128)S(1)}, f32[2,256]{1,0:T(2,128)}, u32[]{:S(2)}) copy-start(f32[2,256]{1,0:T(2,128)} %copy-done.15) | copy-start | bytes 6148
  393.6 24.4 %copy-start.18 = (f32[512]{0:T(512)S(1)}, f32[512]{0:T(512)}, u32[]{:S(2)}) copy-start(f32[512]{0:T(512)} %copy-done.17) | copy-start | bytes 6148
  393.6 24.4 %copy-start.20 = (f32[2,256]{1,0:T(2,128)S(1)}, f32[2,256]{1,0:T(2,128)}, u32[]{:S(2)}) copy-start(f32[2,256]{1,0:T(2,128)} %copy-done.19) | copy-start | bytes 6148
  393.6 50.7 %copy-start.5 = (bf16[2,256,512]{2,1,0:T(8,128)(2,1)S(1)}, bf16[2,256,512]{2,1,0:T(8,128)(2,1)}, u32[]{:S(2)}) copy-start(bf16[2,256,512]{2,1,0:T(8,128)(2,1)} %get-tuple-element.37) | copy-start | bytes 1572868
  393.6 53.0 %copy-start.1 = (bf16[256,512]{1,0:T(8,128)(2,1)S(1)}, bf16[256,512]{1,0:T(8,128)(2,1)}, u32[]{:S(2)}) copy-start(bf16[256,512]{1,0:T(8,128)(2,1)} %param.26) | copy-start | bytes 786436
  (7 other events, 10.6 us)
Sparse Core Ops, SparseCore 0:
  14.1 30.5 all-gather.4
  84.4 33.7 reduce-scatter.4
  121.1 26.5 all-gather.6
  149.2 27.6 all-gather.8
  187.1 33.8 reduce-scatter.8
  223.1 32.6 reduce-scatter.6
  258.9 26.5 all-gather.10
  384.1 33.8 reduce-scatter.10
where the time goes:
time: 462 us; the launch traced here: 454 us
  waiting for transfers between devices  221 us (48%)
  matrix products  167 us (36%)
  blocking collectives  24 us (5%)
  other arithmetic  22.3 us (5%)
  between operations  14.7 us (3%)
    dot_general x1, matrix products, attention_backward(): jnp.einsum('bhqk,bqhe->bkhe', grad_scores, qkv_proj[0], preferred_element...  34.7 us
    reduce_scatter x1, waiting for transfers between devices, device_step(): lax.psum_scatter(attn_part, 'tp', scatter_dimension=1, tiled=True)  33.8 us
    dot_general x1, matrix products, attention_backward(): jnp.einsum('bhqk,bkhe->bqhe', grad_scores, qkv_proj[1], preferred_element...  33.4 us
    reduce_scatter x1, waiting for transfers between devices, device_step(): lax.psum_scatter(mlp_part, 'tp', scatter_dimension=1, tiled=True)  33.2 us
    reduce_scatter x1, waiting for transfers between devices, device_step(): lax.psum_scatter(grad_norm2_part, 'tp', scatter_dimension=1, tiled=True)  28 us
    all_gather x1, waiting for transfers between devices, device_step(): grad_resid1_all = lax.all_gather(grad_resid1, 'tp', axis=1, tiled=True)  26.1 us
    all_gather x1, waiting for transfers between devices, device_step(): normed1_all = lax.all_gather(normed1, 'tp', axis=1, tiled=True)  25.8 us
    all_gather x1, waiting for transfers between devices, device_step(): normed2_all = lax.all_gather(normed2, 'tp', axis=1, tiled=True)  25.8 us
  transfers between devices with their start and end apart: 8, of which 8 were waited for; matrix products, arithmetic and copies ran while one was open for 6% of the time, Pallas kernels for 0%

commit v1 on v0

v1 whole, which is shorter than its diff:
```python
import jax
import jax.numpy as jnp
from jax import lax
from jax.experimental import pallas as pl
from jax.experimental.pallas import tpu as pltpu
from jax.sharding import PartitionSpec as P

LN_EPS = 1e-5
MESH = pl.DeviceIdType.MESH
F32 = jnp.float32
BF16 = jnp.bfloat16
LOG2E = 1.4426950408889634
GELU_A = 0.7978845608028654
GELU_B = 0.044715

W2_ROW, W1_ROW, WO_ROW, WQ_ROW, BU_ROW, W_ROWS, W_CUT = 0, 256, 512, 576, 768, 784, 384
DB_ROW, G_ROWS, G_HALF = 576, 592, 296


def mm(lhs, rhs, lc=1, rc=0):
    return lax.dot_general(lhs, rhs, (((lc,), (rc,)), ((), ())), preferred_element_type=F32)


def norm_stats(value):
    centered = value - jnp.mean(value, axis=-1, keepdims=True)
    inv_std = lax.rsqrt(jnp.mean(centered * centered, axis=-1, keepdims=True) + LN_EPS)
    return centered * inv_std, inv_std


def norm_back(grad, x_hat, inv_std, gain):
    scaled = grad * gain
    return inv_std * (scaled - jnp.mean(scaled, axis=-1, keepdims=True) - x_hat * jnp.mean(scaled * x_hat, axis=-1, keepdims=True))


def layer_kernel(n_dev, attn_scale,
                 x, dy, g1, s1, bo, g2, s2, bd, wqkv, bqkv, wo, wu, bu, wd,
                 y_out, dx_out, vec_out, dwqkv_out, dbqkv_out, dwo_out, dwu_out, dbu_out, dwd_out,
                 h1, wp, q_s, k_s, v_s, qkvt, s_scr, lse, o_own, o_all, wo_all, x1, h2, ga, dza, acc, dx1, do_send, do_all, do_s,
                 delta, dqt, dk_s, dv_s, dqkvt, dqkvt_all, dwp, dwr, r_a, r_b, r_l, r_r, vec, vec_all,
                 ag_ss, ag_rs, o_ss, o_rs, do_ss, do_rs, dq_ss, dq_rs, dw_ss, dw_rs, v_ss, v_rs):
    me = lax.axis_index("tp")
    chips = n_dev // 2
    chip, core = lax.div(me, 2), lax.rem(me, 2)

    def dev(shift, other):
        return 2 * lax.rem(chip + shift + chips, chips) + (1 - core if other else core)

    L, R, O, PT = dev(-1, False), dev(1, False), dev(2, False), dev(0, True)
    PL, PR, PO = dev(-1, True), dev(1, True), dev(2, True)

    def rc(src, dst, ssem, rsem, target):
        return pltpu.make_async_remote_copy(src_ref=src, dst_ref=dst, send_sem=ssem, recv_sem=rsem,
                                            device_id={"tp": target}, device_id_type=MESH)

    def m256(i):
        return pl.ds(pl.multiple_of(i * 256, 256), 256)

    plan = ((me, "F", R, L), (me, "F", L, R), (me, "F", PT, PT), (L, "A", R, O), (R, "B", L, O),
            (L, "F", PT, PL), (R, "F", PT, PR), (O, "A", PT, PO), (O, "B", PT, PO))

    def view(a, owner, part):
        if a < 2:
            off, size = {"F": (0, 256), "A": (0, 128), "B": (128, 128)}[part]
            return h1.at[a, pl.ds(pl.multiple_of(owner * 256 + off, 128), size), :]
        off, size = {"F": (0, W_ROWS), "A": (0, W_CUT), "B": (W_CUT, W_ROWS - W_CUT)}[part]
        return wp.at[owner, pl.ds(off, size), :]

    def ag_copy(a, ch, received):
        own, part, target, got = plan[ch]
        v = view(a, got if received else own, part)
        return rc(v, v, ag_ss.at[a, ch], ag_rs.at[a, ch], target)

    def ag_start(a, *chs):
        for ch in chs:
            ag_copy(a, ch, False).start()

    def ag_wait(a, *chs):
        for ch in chs:
            ag_copy(a, ch, True).wait_recv()

    barrier = pltpu.get_barrier_semaphore()
    for i in range(n_dev):
        @pl.when(me != i)
        def _():
            pl.semaphore_signal(barrier, inc=1, device_id={"tp": i}, device_id_type=MESH)

    gain1, shift1 = g1[...].astype(F32), s1[...].astype(F32)
    for b in range(2):
        for r in range(2):
            rows = slice(b * 256 + r * 128, b * 256 + r * 128 + 128)
            x_hat, _ = norm_stats(x[rows, :].astype(F32))
            h1[b, pl.ds(pl.multiple_of(me * 256 + r * 128, 128), 128), :] = (x_hat * gain1 + shift1).astype(BF16)

    pl.semaphore_wait(barrier, n_dev - 1)
    for b in range(2):
        ag_start(b, 0, 1, 2)

    wp[me, W2_ROW:W1_ROW, :] = wd[...]
    wp[me, W1_ROW:WO_ROW, :] = wu[...].astype(F32).T.astype(BF16)
    wp[me, WO_ROW:WQ_ROW, :] = wo[...]
    wp[me, WQ_ROW:BU_ROW, :] = wqkv[...].astype(F32).T[:192, :].astype(BF16)
    wp[me, BU_ROW:W_ROWS, 0:256] = jnp.broadcast_to(bu[...].astype(F32), (16, 256)).astype(BF16)
    wp[me, BU_ROW:W_ROWS, 256:512] = jnp.zeros((16, 256), BF16)

    bias_qkv = bqkv[...].astype(F32)

    def project(b, owner):
        rows = m256(owner)
        full = (mm(h1[b, rows, :], wqkv[...]) + bias_qkv).astype(BF16).astype(F32)
        q_s[b, rows, :] = full[:, 0:64].astype(BF16)
        k_s[b, rows, :] = full[:, 64:128].astype(BF16)
        v_s[b, rows, :] = full[:, 128:192].astype(BF16)
        qkvt[b, :, rows] = full.T[:192, :].astype(BF16)

    for b in range(2):
        project(b, me)
    for b in range(2):
        ag_wait(b, 0)
        ag_start(b, 3, 5)
        ag_wait(b, 1)
        ag_start(b, 4, 6)
        ag_wait(b, 2)
        if b == 1:
            ag_start(2, 0, 1, 2)
        for owner in (PT, L, R):
            project(b, owner)

    s_fac = attn_scale * LOG2E

    def causal(shape):
        return lax.broadcasted_iota(jnp.int32, shape, 0) <= lax.broadcasted_iota(jnp.int32, shape, 1)

    def o_copy(b, j, src):
        lanes = pl.ds(b * 256, 256)
        return rc(o_own.at[b, :, m256(j)], o_all.at[pl.ds(pl.multiple_of(src * 64, 64), 64), lanes],
                  o_ss.at[b, j], o_rs.at[b, src], j)

    def attend(b, j):
        cols = m256(j)
        q_t = qkvt[b, 0:64, cols]

        def scores(kc, m):
            s = mm(k_s[b, m256(kc), :], q_t) * s_fac
            s_scr[m256(kc), :] = s
            return jnp.maximum(m, jnp.max(s, axis=0, keepdims=True))

        s_d = jnp.where(causal((256, 256)), mm(k_s[b, cols, :], q_t) * s_fac, -1e30)
        s_scr[cols, :] = s_d
        m = lax.fori_loop(0, j, scores, jnp.max(s_d, axis=0, keepdims=True))

        def sums(kc, l):
            return l + jnp.sum(jnp.exp2(s_scr[m256(kc), :] - m), axis=0, keepdims=True)

        l = lax.fori_loop(0, j + 1, sums, jnp.zeros((1, 256), F32))
        lse_j = m + jnp.log2(l)
        lse[b, :, cols] = lse_j

        def outs(kc, o):
            p = jnp.exp2(s_scr[m256(kc), :] - lse_j).astype(BF16)
            return o + mm(qkvt[b, 128:192, m256(kc)], p)

        o = lax.fori_loop(0, j + 1, outs, jnp.zeros((64, 256), F32)).astype(BF16)
        o_own[b, :, cols] = o

        @pl.when(j != me)
        def _():
            o_copy(b, j, me).start()

        @pl.when(j == me)
        def _():
            o_all[pl.ds(pl.multiple_of(me * 64, 64), 64), pl.ds(b * 256, 256)] = o

    for b in range(2):
        ag_wait(b, 3)
        ag_start(b, 7)
        ag_wait(b, 4)
        ag_start(b, 8)
        project(b, O)
        ag_wait(b, 5, 6)
        project(b, PL)
        project(b, PR)
        ag_wait(b, 7, 8)
        project(b, PO)

        @pl.loop(0, n_dev)
        def _(j):
            attend(b, j)

    ag_wait(2, 0)
    ag_start(2, 3, 5)
    ag_wait(2, 1)
    ag_start(2, 4, 6)
    ag_wait(2, 2, 5, 6, 3)
    ag_start(2, 7)
    ag_wait(2, 4)
    ag_start(2, 8)
    ag_wait(2, 7, 8)
    for n in range(n_dev):
        wo_all[n * 64:(n + 1) * 64, :] = wp[n, WO_ROW:WQ_ROW, :]
    for b in range(2):
        for src in range(n_dev):
            @pl.when(me != src)
            def _():
                o_copy(b, me, src).wait_recv()

    bias_o = bo[...].astype(F32)
    gain2, shift2 = g2[...].astype(F32), s2[...].astype(F32)
    for r in range(4):
        rows = slice(r * 128, r * 128 + 128)
        attn = mm(o_all[:, rows], wo_all[...], 0, 0)
        x1_r = (x[rows, :].astype(F32) + attn + bias_o).astype(BF16)
        x1[rows, :] = x1_r
        x_hat, _ = norm_stats(x1_r.astype(F32))
        h2[rows, :] = (x_hat * gain2 + shift2).astype(BF16)
    acc[...] = jnp.zeros_like(acc)

    @pl.loop(0, n_dev)
    def _(n):
        w1t = wp[n, W1_ROW:WO_ROW, :]
        w2 = wp[n, W2_ROW:W1_ROW, :]
        bias_u = wp[n, BU_ROW:W_ROWS, 0:256].astype(F32)[0:1, :]
        for r in range(2):
            rows = slice(r * 256, r * 256 + 256)
            z = (mm(h2[rows, :], w1t, 1, 1) + bias_u).astype(BF16).astype(F32)
            z2 = z * z
            t = jnp.tanh(GELU_A * (z + GELU_B * z2 * z))
            ga[n, rows, :] = (0.5 * z * (1.0 + t)).astype(BF16)
            slope = 0.5 * (1.0 + t) + 0.5 * z * (1.0 - t * t) * (GELU_A * (1.0 + 3.0 * GELU_B * z2))
            dgl = mm(dy[rows, :], w2, 1, 1).astype(BF16).astype(F32)
            dz = (dgl * slope).astype(BF16)
            dza[n, rows, :] = dz
            acc[rows, :] += mm(dz, w1t)

    vec[...] = jnp.zeros_like(vec)
    for r in range(4):
        rows = slice(r * 128, r * 128 + 128)
        dh2 = acc[rows, :].astype(BF16).astype(F32)
        x_hat, inv_std = norm_stats(x1[rows, :].astype(F32))
        dy_r = dy[rows, :].astype(F32)
        dx1_r = (dy_r + norm_back(dh2, x_hat, inv_std, gain2)).astype(BF16)
        dx1[rows, :] = dx1_r
        vec[2:3, :] += jnp.sum(dx1_r.astype(F32), axis=0, keepdims=True)
        vec[3:4, :] += jnp.sum(dh2 * x_hat, axis=0, keepdims=True)
        vec[4:5, :] += jnp.sum(dh2, axis=0, keepdims=True)
        vec[5:6, :] += jnp.sum(dy_r, axis=0, keepdims=True)

    def do_copy(n, src):
        return rc(do_send.at[pl.ds(pl.multiple_of(n * 64, 64), 64), :], do_all.at[src], do_ss.at[n], do_rs.at[src], n)

    for r in range(2):
        rows = slice(r * 256, r * 256 + 256)
        do_send[rows, :] = mm(wo_all[rows, :], dx1[...], 1, 1).astype(BF16)
    for n in range(n_dev):
        @pl.when(me != n)
        def _():
            do_copy(n, me).start()
    do_all[me] = do_send[pl.ds(pl.multiple_of(me * 64, 64), 64), :]

    def grads(n):
        for r in range(2):
            cols = slice(r * 128, r * 128 + 128)
            dwp[n, W2_ROW + r * 128:W2_ROW + r * 128 + 128, :] = mm(ga[n, :, cols], dy[...], 0, 0)
            dwp[n, W1_ROW + r * 128:W1_ROW + r * 128 + 128, :] = mm(dza[n, :, cols], h2[...], 0, 0)
        dwp[n, WO_ROW:DB_ROW, :] = mm(o_all[pl.ds(pl.multiple_of(n * 64, 64), 64), :], dx1[...])
        dwp[n, DB_ROW:G_ROWS, 0:256] = jnp.broadcast_to(
            jnp.sum(dza[n].astype(F32), axis=0, keepdims=True), (G_ROWS - DB_ROW, 256))
        dwp[n, DB_ROW:G_ROWS, 256:512] = jnp.zeros((G_ROWS - DB_ROW, 256), F32)

    def pair_copy(i):
        return rc(dwp.at[2 * i + 1 - core], dwr.at[i], dw_ss.at[i], dw_rs.at[i], PT)

    @pl.loop(0, chips)
    def _(i):
        grads(2 * i + 1 - core)
        pair_copy(i).start()

    @pl.loop(0, chips)
    def _(i):
        grads(2 * i + core)

    acc[...] = jnp.zeros_like(acc)

    @pl.loop(0, n_dev)
    def _(n):
        for r in range(2):
            rows = slice(r * 256, r * 256 + 256)
            acc[rows, :] += mm(ga[n, rows, :], wp[n, W2_ROW:W1_ROW, :])

    y_out[...] = (x1[...].astype(F32) + acc[...] + bd[...].astype(F32)).astype(BF16)

    @pl.loop(0, chips)
    def _(i):
        pair_copy(i).wait_recv()
        dwp[2 * i + core] += dwr[i]

    top, low = pl.ds(0, G_HALF), pl.ds(G_HALF, G_HALF)

    def ring_copy(step):
        src, dst, target = (
            (dwp.at[O, top, :], r_a, R), (dwp.at[O, low, :], r_b, L), (dwp.at[R], r_l, R), (dwp.at[L], r_r, L))[step]
        return rc(src, dst, dw_ss.at[chips + step], dw_rs.at[chips + step], target)

    ring_copy(0).start()
    ring_copy(1).start()

    for j in range(n_dev):
        @pl.when(me != j)
        def _():
            do_copy(me, j).wait_recv()
        for b in range(2):
            do_t = do_all[j, :, b * 256:(b + 1) * 256].astype(F32)
            do_s[b, j * 256:(j + 1) * 256, :] = do_t.T.astype(BF16)
            delta[b, :, j * 256:(j + 1) * 256] = jnp.sum(
                do_t * o_own[b, :, j * 256:(j + 1) * 256].astype(F32), axis=0, keepdims=True)
    dqt[...] = jnp.zeros_like(dqt)
    dwqkv_out[...] = jnp.zeros_like(dwqkv_out)
    dbqkv_out[...] = jnp.zeros_like(dbqkv_out)

    def dq_copy(b, j, src):
        lanes = pl.ds(b * 256, 256)
        return rc(dqkvt.at[b, :, m256(j)], dqkvt_all.at[src, :, lanes], dq_ss.at[b, j], dq_rs.at[b, src], j)

    def tile(b, kb, qb, masked):
        rows, cols = m256(kb), m256(qb)
        s = mm(k_s[b, rows, :], qkvt[b, 0:64, cols]) * s_fac
        p = jnp.exp2(s - lse[b, :, cols])
        if masked:
            p = jnp.where(causal((256, 256)), p, 0.0)
        dp = mm(v_s[b, rows, :], do_all[qb, :, b * 256:(b + 1) * 256]).astype(BF16).astype(F32)
        ds = (p * (dp - delta[b, :, cols]) * attn_scale).astype(BF16)
        dv = mm(p.astype(BF16), do_s[b, cols, :])
        dk = mm(ds, q_s[b, cols, :])
        dqt[b, :, cols] += mm(qkvt[b, 64:128, rows], ds)
        if masked:
            dv_s[b] = dv
            dk_s[b] = dk
        else:
            dv_s[b] += dv
            dk_s[b] += dk

    @pl.loop(0, n_dev)
    def _(kb):
        @pl.when(kb == 3)
        def _():
            ring_copy(0).wait_recv()
            dwp[R, top, :] += r_a[...]
            ring_copy(2).start()
            ring_copy(1).wait_recv()
            dwp[L, low, :] += r_b[...]
            ring_copy(3).start()

        for b in range(2):
            tile(b, kb, kb, True)

        @pl.loop(kb + 1, n_dev)
        def _(qb):
            for b in range(2):
                tile(b, kb, qb, False)

        cols = m256(kb)
        for b in range(2):
            dkv_t = jnp.concatenate([dk_s[b], dv_s[b]], axis=1).T
            dqkvt[b, 0:64, cols] = dqt[b, :, cols].astype(BF16)
            dqkvt[b, 64:192, cols] = dkv_t.astype(BF16)

            @pl.when(kb != me)
            def _():
                dq_copy(b, kb, me).start()

            blk = dqkvt[b, :, cols]

            @pl.when(kb == me)
            def _():
                dqkvt_all[me, :, b * 256:(b + 1) * 256] = blk

            dwqkv_out[...] += mm(blk, h1[b, cols, :])
            dbqkv_out[...] += mm(jnp.ones((8, 256), BF16), blk, 1, 1)

    ring_copy(2).wait_recv()
    ring_copy(3).wait_recv()
    dwd_out[...] = dwp[me, W2_ROW:W1_ROW, :] + r_l[W2_ROW:W1_ROW, :] + r_r[W2_ROW:W1_ROW, :]
    dwu_out[...] = (dwp[me, W1_ROW:WO_ROW, :] + r_l[W1_ROW:WO_ROW, :] + r_r[W1_ROW:WO_ROW, :]).T
    dwo_out[...] = dwp[me, WO_ROW:DB_ROW, :] + r_l[WO_ROW:DB_ROW, :] + r_r[WO_ROW:DB_ROW, :]
    dbu_out[...] = dwp[me, DB_ROW:DB_ROW + 8, 0:256] + r_l[DB_ROW:DB_ROW + 8, 0:256] + r_r[DB_ROW:DB_ROW + 8, 0:256]

    for b in range(2):
        for src in range(n_dev):
            @pl.when(me != src)
            def _():
                dq_copy(b, me, src).wait_recv()
    acc[...] = jnp.zeros_like(acc)

    @pl.loop(0, n_dev)
    def _(n):
        for r in range(2):
            rows = slice(r * 256, r * 256 + 256)
            acc[rows, :] += mm(dqkvt_all[n, :, rows], wp[n, WQ_ROW:BU_ROW, :], 0, 0)

    for r in range(4):
        rows = slice(r * 128, r * 128 + 128)
        dh1 = acc[rows, :].astype(BF16).astype(F32)
        x_hat, inv_std = norm_stats(x[rows, :].astype(F32))
        dx_out[rows, :] = (dx1[rows, :].astype(F32) + norm_back(dh1, x_hat, inv_std, gain1)).astype(BF16)
        vec[0:1, :] += jnp.sum(dh1 * x_hat, axis=0, keepdims=True)
        vec[1:2, :] += jnp.sum(dh1, axis=0, keepdims=True)

    def vec_copy(j, src):
        return rc(vec, vec_all.at[src], v_ss.at[j], v_rs.at[src], j)

    for j in range(n_dev):
        @pl.when(me != j)
        def _():
            vec_copy(j, me).start()
    vec_all[me] = vec[...]
    for j in range(n_dev):
        @pl.when(me != j)
        def _():
            vec_copy(me, j).wait_recv()
    total = vec_all[0]
    for j in range(1, n_dev):
        total = total + vec_all[j]
    vec_out[...] = total

    for a in range(3):
        for ch in range(9):
            ag_copy(a, ch, False).wait_send()
    for i in range(chips):
        pair_copy(i).wait_send()
    for step in range(4):
        ring_copy(step).wait_send()
    for j in range(n_dev):
        @pl.when(me != j)
        def _():
            do_copy(j, me).wait_send()
            vec_copy(j, me).wait_send()
            for b in range(2):
                o_copy(b, j, me).wait_send()
                dq_copy(b, j, me).wait_send()


def solution(mesh):
    n_dev = mesh.shape["tp"]

    def device_step(hidden, grad_out, ln1_gain, ln1_bias, w_qkv, b_qkv, w_out, b_out, ln2_gain, ln2_bias, w_up, b_up, w_down, b_down):
        batch, tokens, d = hidden.shape
        rows = batch * tokens
        head = w_qkv.shape[-1]
        seq = tokens * n_dev
        ff = w_up.shape[1]
        attn_scale = head ** -0.5
        row = lambda v: v.reshape(1, -1)
        wq = jnp.pad(w_qkv.reshape(d, 3 * head), ((0, 0), (0, 256 - 3 * head)))
        bq = jnp.pad(b_qkv.reshape(1, 3 * head), ((0, 0), (0, 256 - 3 * head)))
        sds = jax.ShapeDtypeStruct
        vm = pltpu.VMEM
        dma = pltpu.SemaphoreType.DMA
        outs = pl.pallas_call(
            lambda *refs: layer_kernel(n_dev, attn_scale, *refs),
            out_shape=(sds((rows, d), BF16), sds((rows, d), BF16), sds((8, d), F32), sds((3 * head, d), F32), sds((8, 3 * head), F32),
                       sds((head, d), F32), sds((d, ff), F32), sds((8, ff), F32), sds((ff, d), F32)),
            in_specs=[pl.BlockSpec(memory_space=pltpu.VMEM)] * 14,
            out_specs=tuple([pl.BlockSpec(memory_space=pltpu.VMEM)] * 9),
            scratch_shapes=[
                vm((2, seq, d), BF16), vm((n_dev, W_ROWS, d), BF16),
                vm((2, seq, head), BF16), vm((2, seq, head), BF16), vm((2, seq, head), BF16), vm((2, 3 * head, seq), BF16),
                vm((seq, 256), F32), vm((2, 1, seq), F32), vm((2, head, seq), BF16), vm((n_dev * head, rows), BF16),
                vm((n_dev * head, d), BF16), vm((rows, d), BF16), vm((rows, d), BF16),
                vm((n_dev, rows, ff), BF16), vm((n_dev, rows, ff), BF16), vm((rows, d), F32), vm((rows, d), BF16),
                vm((n_dev * head, rows), BF16), vm((n_dev, head, rows), BF16), vm((2, seq, head), BF16),
                vm((2, 1, seq), F32), vm((2, head, seq), F32), vm((2, 256, head), F32), vm((2, 256, head), F32),
                vm((2, 3 * head, seq), BF16), vm((n_dev, 3 * head, rows), BF16),
                vm((n_dev, G_ROWS, d), F32), vm((n_dev // 2, G_ROWS, d), F32),
                vm((G_HALF, d), F32), vm((G_HALF, d), F32), vm((G_ROWS, d), F32), vm((G_ROWS, d), F32),
                vm((8, d), F32), vm((n_dev, 8, d), F32),
                dma((3, 9)), dma((3, 9)), dma((2, n_dev)), dma((2, n_dev)), dma((n_dev,)), dma((n_dev,)),
                dma((2, n_dev)), dma((2, n_dev)), dma((n_dev // 2 + 4,)), dma((n_dev // 2 + 4,)), dma((n_dev,)), dma((n_dev,)),
            ],
            compiler_params=pltpu.CompilerParams(collective_id=0, has_side_effects=True, vmem_limit_bytes=67043328),
            name="layer",
        )(hidden.reshape(rows, d), grad_out.reshape(rows, d), row(ln1_gain), row(ln1_bias), row(b_out), row(ln2_gain), row(ln2_bias),
          row(b_down), wq, bq, w_out.reshape(head, d), w_up, row(b_up), w_down)
        y, dx, vec, dwqkv_t, dbqkv, dwo, dwu, dbu, dwd = outs
        return (y.reshape(hidden.shape), dx.reshape(hidden.shape), vec[0], vec[1], dwqkv_t.T.reshape(w_qkv.shape),
                dbqkv[0].reshape(b_qkv.shape), dwo.reshape(w_out.shape), vec[2], vec[3], vec[4], dwu, dbu[0], dwd, vec[5])

    act_spec = P("dp", "tp", None)
    vec_spec = P(None)
    group_vec = P("dp")
    in_specs = (act_spec, act_spec, vec_spec, vec_spec, P(None, None, "tp", None), P(None, "tp", None), P("tp", None, None), vec_spec, vec_spec, vec_spec, P(None, "tp"), P("tp"), P("tp", None), vec_spec)
    out_specs = (act_spec, act_spec, group_vec, group_vec, P("dp", None, "tp", None), P("dp", "tp", None), P(("dp", "tp"), None, None), group_vec, group_vec, group_vec, P("dp", "tp"), P(("dp", "tp")), P(("dp", "tp"), None), group_vec)
    return jax.shard_map(device_step, mesh=mesh, in_specs=in_specs, out_specs=out_specs, check_vma=False)
```

time: 462 us -> 183 us (0.40)
  the two profiles are of different devices: /device:TPU:112 before, /device:TPU:121 now
where the time goes in v1:
time: 183 us; the launch traced here: 182 us
  Pallas kernels  163 us (89%)
  local copies, waits for them, and re-layouts  18.1 us (10%)
    pallas_call x1, Pallas kernels, device_step(): pl.pallas_call(lambda *refs: layer_kernel(n_dev, attn_scale, *refs), out_...  163 us
    unnamed x32, local copies, waits for them, and re-layouts  7.48 us
    reshape x7, local copies, waits for them, and re-layouts, device_step(): row = lambda v: v.reshape(1, -1)  4.05 us

profile of v1, /device:TPU:121, one launch (start us, length us, event | category | flops | bytes accessed | tf_op | source)
XLA Modules:
  0.0 182.2 jit_solution(17941373018624798708)
XLA Ops:
  0.6 1.1 copy.31
  1.7 0.7 pad.8.refs_8_
  2.5 0.1 reshape.85
  2.6 0.6 pad.9.refs_9_
  3.1 0.1 copy-done.5
  3.2 0.6 reshape.78.refs_2_
  3.8 0.1 copy-done.6
  3.9 0.6 reshape.79.refs_3_
  4.5 0.1 copy-done.7
  4.6 0.6 reshape.80.refs_4_
  5.2 0.1 copy-done.8
  5.3 0.6 reshape.81.refs_5_
  5.9 0.1 copy-done.9
  6.0 0.6 reshape.82.refs_6_
  6.5 0.1 copy-done.10
  6.6 0.6 reshape.83.refs_7_
  7.2 0.1 copy-done.12
  7.3 0.6 reshape.87.refs_12_
  7.9 163.3 %layer.1 = (bf16[512,512]{1,0:T(8,128)(2,1)}, bf16[512,512]{1,0:T(8,128)(2,1)}, f32[8,512]{1,0:T(8,128)}, f32[192,512]{1,0:T(8,128)}, f32[8,192]{1,0:T(8,128)}, ...) custom-call(bf16[512,512]{1,0:T(8,128)(2,1)} %bitcast.21, ...), custom_call_target="tpu_custom_call" | custom-call | tf_op jit(solution)/shard_map/layer/pallas_call | solution.py:457
  171.2 1.5 fusion
  172.7 0.7 slice_reduce_fusion
  173.5 0.6 reshape_squeeze.4
  174.1 1.3 slice.30
  175.4 1.9 %copy.40 = bf16[2,256,512]{2,1,0:T(8,128)(2,1)} copy(bf16[2,256,512]{2,1,0:T(8,128)(2,1)} %bitcast.24) | data formatting | bytes 1048576
  177.3 0.8 copy.41
  178.1 0.4 copy-done.3
  178.5 0.7 copy.42
  179.2 0.2 copy-done.4
  179.5 0.7 copy.43
  180.1 0.8 copy.44
  180.9 0.4 copy-done
  181.4 0.8 copy.45
  (16 shorter events, 0.0 us)
Async XLA Ops:
  1.7 0.8 copy-start.11
  2.5 0.7 copy-start.5
  3.2 0.7 copy-start.6
  3.9 0.7 copy-start.7
  4.6 0.7 copy-start.8
  5.3 0.7 copy-start.9
  6.0 0.7 copy-start.10
  6.6 0.7 copy-start.12
  175.4 1.9 %copy-start.2 = (bf16[512,512]{1,0:T(8,128)(2,1)S(1)}, bf16[512,512]{1,0:T(8,128)(2,1)}, u32[]{:S(2)}) copy-start(bf16[512,512]{1,0:T(8,128)(2,1)} %get-tuple-element.24) | copy-start | bytes 1572868
  177.3 1.2 copy-start.3
  178.5 1.0 copy-start.4
  178.5 1.7 copy-start.1
  180.1 1.2 copy-start

commit v2 on v0

v2 whole, which is shorter than its diff:
```python
import jax
import jax.numpy as jnp
from jax import lax
from jax.experimental import pallas as pl
from jax.experimental.pallas import tpu as pltpu
from jax.sharding import PartitionSpec as P

LN_EPS = 1e-5
MESH = pl.DeviceIdType.MESH
F32 = jnp.float32
BF16 = jnp.bfloat16
LOG2E = 1.4426950408889634
GELU_A = 0.7978845608028654
GELU_B = 0.044715

W_ROWS, WO_ROWS = 512, 80
GB_ROWS = 336


def mm(lhs, rhs, lc=1, rc=0):
    return lax.dot_general(lhs, rhs, (((lc,), (rc,)), ((), ())), preferred_element_type=F32)


def norm_stats(value):
    centered = value - jnp.mean(value, axis=-1, keepdims=True)
    inv_std = lax.rsqrt(jnp.mean(centered * centered, axis=-1, keepdims=True) + LN_EPS)
    return centered * inv_std, inv_std


def norm_back(grad, x_hat, inv_std, gain):
    scaled = grad * gain
    return inv_std * (scaled - jnp.mean(scaled, axis=-1, keepdims=True) - x_hat * jnp.mean(scaled * x_hat, axis=-1, keepdims=True))


def vector(ref):
    return ref[...].astype(F32).reshape(1, -1)


def layer_kernel(n_dev, attn_scale,
                 x, dy, g1, s1, bo, g2, s2, bd, wqkv, bqkv, wo, wu, bu, wd,
                 y_out, dx_out, vec_out, dwqkv_out, dwo_out, dwu_out, dbu_out, dwd_out,
                 h1own, h1, wob, wp, wqp, wq, q_s, k_s, v_s, qkvt, big, lse, o_own, o_all, wo_all, x1, h2, ga, dza, acc, dx1,
                 do_send, do_all, do_s, delta, dqt, dqkvt, dh_send, dh_pair, dh_all, dwq, dwq_r,
                 dwa, dwb, pra, prb, ra_a, ra_b, ra_l, ra_r, rb_a, rb_b, rb_l, rb_r, vec, vec_all,
                 hs_ss, hs_rs, hp_ss, hp_rs, wq_ss, wq_rs, ag_ss, ag_rs, o_ss, o_rs, do_ss, do_rs, dhp_ss, dhp_rs, dh_ss, dh_rs,
                 pr_ss, pr_rs, rg_ss, rg_rs, v_ss, v_rs):
    me = lax.axis_index("tp")
    chips = n_dev // 2
    chip, core = lax.div(me, 2), lax.rem(me, 2)
    seq = lax.div(chip, chips // 2)
    mate = 2 * (chips - 1 - chip) + core

    def dev(shift, other):
        return 2 * lax.rem(chip + shift + chips, chips) + (1 - core if other else core)

    L, R, O, PT = dev(-1, False), dev(1, False), dev(2, False), dev(0, True)
    PL, PR, PO = dev(-1, True), dev(1, True), dev(2, True)

    def handler(n, st):
        return n if (n // 2) // (chips // 2) == st else 2 * (chips - 1 - n // 2) + n % 2

    def rc(src, dst, ssem, rsem, target):
        return pltpu.make_async_remote_copy(src_ref=src, dst_ref=dst, send_sem=ssem, recv_sem=rsem,
                                            device_id={"tp": target}, device_id_type=MESH)

    def m256(i):
        return pl.ds(i * 256, 256) if isinstance(i, int) else pl.ds(pl.multiple_of(i * 256, 256), 256)

    def m64(i):
        return pl.ds(i * 64, 64) if isinstance(i, int) else pl.ds(pl.multiple_of(i * 64, 64), 64)

    plan = ((me, "F", R, L), (me, "F", L, R), (me, "F", PT, PT), (L, "A", R, O), (R, "B", L, O),
            (L, "F", PT, PL), (R, "F", PT, PR), (O, "A", PT, PO), (O, "B", PT, PO))

    def view(a, owner, part):
        cut, rows = ((48, WO_ROWS), (256, W_ROWS))[a]
        off, size = {"F": (0, rows), "A": (0, cut), "B": (cut, rows - cut)}[part]
        return (wob, wp)[a].at[owner, pl.ds(off, size), :]

    def ag_copy(a, ch, received):
        own, part, target, got = plan[ch]
        v = view(a, got if received else own, part)
        return rc(v, v, ag_ss.at[a, ch], ag_rs.at[a, ch], target)

    def ag_start(a, *chs):
        for ch in chs:
            ag_copy(a, ch, False).start()

    def ag_wait(a, *chs):
        for ch in chs:
            ag_copy(a, ch, True).wait_recv()

    barrier = pltpu.get_barrier_semaphore()
    for i in range(n_dev):
        @pl.when(me != i)
        def _():
            pl.semaphore_signal(barrier, inc=1, device_id={"tp": i}, device_id_type=MESH)

    gain1, shift1 = vector(g1), vector(s1)
    for b in range(2):
        for r in range(2):
            rows = slice(b * 256 + r * 128, b * 256 + r * 128 + 128)
            x_hat, _ = norm_stats(x[rows, :].astype(F32))
            h1own[b, r * 128:r * 128 + 128, :] = (x_hat * gain1 + shift1).astype(BF16)
    h1[m256(me), :] = h1own[seq]
    wqp[0, 0:192, :] = wqkv[...]
    bq_row = jnp.concatenate([bqkv[c].astype(F32) for c in range(3)] + [jnp.zeros((1, 320), F32)], axis=1)
    wqp[0, 192:208, :] = jnp.broadcast_to(bq_row, (16, 512)).astype(BF16)

    def h1_send(t):
        return rc(h1own.at[t // (chips // 2)], h1.at[m256(me), :], hs_ss.at[t], hs_rs.at[chip], 2 * t + core)

    def h1_recv(src):
        return rc(h1own.at[0], h1.at[m256(2 * src + core), :], hs_ss.at[0], hs_rs.at[src], PT)

    def h1_pair(src, received):
        rows = m256(2 * src + (1 - core if received else core))
        return rc(h1.at[rows, :], h1.at[rows, :], hp_ss.at[src], hp_rs.at[src], PT)

    def wq_copy():
        return rc(wqp.at[0], wqp.at[1], wq_ss.at[0], wq_rs.at[0], mate)

    pl.semaphore_wait(barrier, n_dev - 1)
    wq_copy().start()
    for t in range(chips):
        @pl.when(chip != t)
        def _():
            h1_send(t).start()
    h1_pair(chip, False).start()

    wob[me, 0:64, :] = wo[...]
    wob[me, 64:80, 0:256] = jnp.broadcast_to(vector(bu), (16, 256)).astype(BF16)
    wob[me, 64:80, 256:512] = jnp.zeros((16, 256), BF16)
    wp[me, 0:256, :] = wd[...]
    wp[me, 256:512, :] = wu[...].astype(F32).T.astype(BF16)

    def natural(hi):
        full = jnp.concatenate([wqp[hi, 0:192, :].astype(F32), jnp.zeros((64, 512), F32)], axis=0)
        wq[:, hi * 256:(hi + 1) * 256] = full.T.astype(BF16)

    natural(0)
    wq_copy().wait_recv()
    natural(1)
    bias_qkv = jnp.concatenate([wqp[hi, 192:208, 0:256].astype(F32)[0:1, :] for hi in range(2)], axis=1)

    def project(owner):
        rows = m256(owner)
        full = (mm(h1[rows, :], wq[...]) + bias_qkv).astype(BF16).astype(F32)
        for hi in range(2):
            part = full[:, hi * 256:(hi + 1) * 256]
            q_s[hi, rows, :] = part[:, 0:64].astype(BF16)
            k_s[hi, rows, :] = part[:, 64:128].astype(BF16)
            v_s[hi, rows, :] = part[:, 128:192].astype(BF16)
            qkvt[hi, :, rows] = part.T[:192, :].astype(BF16)

    @pl.loop(0, chips)
    def _(t):
        src = lax.rem(chip + t + lax.div(t, 2) - 2 * lax.div(t, 3), chips)

        @pl.when(t > 0)
        def _():
            h1_recv(src).wait_recv()
            h1_pair(src, False).start()

        project(2 * src + core)
        h1_pair(src, True).wait_recv()
        project(2 * src + 1 - core)

    for a in range(2):
        ag_start(a, 0, 1, 2)

    s_fac = attn_scale * LOG2E
    keep = lax.broadcasted_iota(jnp.int32, (256, 256), 0) <= lax.broadcasted_iota(jnp.int32, (256, 256), 1)

    def o_copy(hi, j):
        head = me + hi * (mate - me)
        return rc(o_own.at[hi, :, m256(j)], o_all.at[m64(head), m256(seq)], o_ss.at[hi, j], o_rs.at[seq, head], j)

    def fold(value, op):
        return op(value.reshape(32, 8, 256), axis=0)

    def attend(hi, j):
        cols = m256(j)
        q_t = qkvt[hi, 0:64, cols]
        base = 8 * (j % 2)
        m = jnp.full((8, 256), -1e30, F32)
        for kc in range(j + 1):
            s = mm(k_s[hi, m256(kc), :], q_t) * s_fac
            if kc == j:
                s = jnp.where(keep, s, -1e30)
            big[base + kc] = s
            m = jnp.maximum(m, fold(s, jnp.max))
        m = jnp.max(m, axis=0, keepdims=True)
        l = jnp.zeros((8, 256), F32)
        for kc in range(j + 1):
            l = l + fold(jnp.exp2(big[base + kc] - m), jnp.sum)
        lse_j = m + jnp.log2(jnp.sum(l, axis=0, keepdims=True))
        lse[hi, :, cols] = lse_j
        o = jnp.zeros((64, 256), F32)
        for kc in range(j + 1):
            p = jnp.exp2(big[base + kc] - lse_j).astype(BF16)
            o = o + mm(qkvt[hi, 128:192, m256(kc)], p)
        o = o.astype(BF16)
        o_own[hi, :, cols] = o

        @pl.when(me != j)
        def _():
            o_copy(hi, j).start()

        @pl.when(me == j)
        def _():
            o_all[m64(me + hi * (mate - me)), m256(seq)] = o

    @pl.loop(0, 2)
    def _(hi):
        @pl.when(hi == 1)
        def _():
            ag_wait(0, 0, 1, 2)
            ag_start(0, 3, 4, 5, 6)

        for j in range(n_dev):
            attend(hi, j)

    ag_wait(1, 0)
    ag_start(1, 3, 5)
    ag_wait(1, 1)
    ag_start(1, 4, 6)
    ag_wait(0, 3, 4)
    ag_start(0, 7, 8)
    ag_wait(0, 5, 6, 7, 8)
    for n in range(n_dev):
        wo_all[n * 64:(n + 1) * 64, :] = wob[n, 0:64, :]
    for st in range(2):
        for n in range(n_dev):
            @pl.when(me != handler(n, st))
            def _():
                rc(o_own.at[0, :, m256(0)], o_all.at[m64(n), m256(st)], o_ss.at[0, 0], o_rs.at[st, n], PT).wait_recv()

    bias_o = vector(bo)
    gain2, shift2 = vector(g2), vector(s2)
    for r in range(4):
        rows = slice(r * 128, r * 128 + 128)
        attn = mm(o_all[:, rows], wo_all[...], 0, 0)
        x1_r = (x[rows, :].astype(F32) + attn + bias_o).astype(BF16)
        x1[rows, :] = x1_r
        x_hat, _ = norm_stats(x1_r.astype(F32))
        h2[rows, :] = (x_hat * gain2 + shift2).astype(BF16)
    acc[...] = jnp.zeros_like(acc)

    packs = ((dwa, pra, ra_a, ra_b, ra_l, ra_r, 128), (dwb, prb, rb_a, rb_b, rb_l, rb_r, GB_ROWS // 2))

    def pair_copy(g, slot):
        return rc(packs[g][0].at[2 * slot + 1 - core], packs[g][1].at[slot], pr_ss.at[g, slot], pr_rs.at[g, slot], PT)

    def pair_add(g, slot):
        pair_copy(g, slot).wait_recv()
        packs[g][0][2 * slot + core] += packs[g][1][slot]

    def ring_copy(g, step):
        pack, _, r_a, r_b, r_l, r_r, half = packs[g]
        top, low = pl.ds(0, half), pl.ds(half, half)
        src, dst, target = (
            (pack.at[O, top, :], r_a, R), (pack.at[O, low, :], r_b, L), (pack.at[R], r_l, R), (pack.at[L], r_r, L))[step]
        return rc(src, dst, rg_ss.at[g, step], rg_rs.at[g, step], target)

    def ring_begin(g):
        pair_add(g, lax.rem(chip + 2, chips))
        ring_copy(g, 0).start()
        ring_copy(g, 1).start()
        for shift in (1, 3, 0):
            pair_add(g, lax.rem(chip + shift, chips))

    def ring_turn(g):
        pack, _, r_a, r_b, _, _, half = packs[g]
        ring_copy(g, 0).wait_recv()
        pack[R, 0:half, :] += r_a[...]
        ring_copy(g, 2).start()
        ring_copy(g, 1).wait_recv()
        pack[L, half:2 * half, :] += r_b[...]
        ring_copy(g, 3).start()

    @pl.loop(0, n_dev)
    def _(i):
        t, other = lax.div(i, 2), lax.rem(i, 2)
        slot = lax.rem(chip + t + lax.div(t, 2) - 2 * lax.div(t, 3), chips)
        n = 2 * slot + core + other * (1 - 2 * core)

        @pl.when(i == 1)
        def _():
            ag_wait(1, 2)

        @pl.when(i == 3)
        def _():
            ag_wait(1, 6)

        @pl.when(i == 5)
        def _():
            ag_wait(1, 5)

        @pl.when(i == 6)
        def _():
            ag_wait(1, 3)
            ag_start(1, 7)
            ag_wait(1, 4)
            ag_start(1, 8)

        @pl.when(i == 7)
        def _():
            ag_wait(1, 7, 8)

        w2 = wp[n, 0:256, :]
        w1t = wp[n, 256:512, :]
        bias_u = wob[n, 64:80, 0:256].astype(F32)[0:1, :]
        for r in range(2):
            rows = slice(r * 256, r * 256 + 256)
            z = (mm(h2[rows, :], w1t, 1, 1) + bias_u).astype(BF16).astype(F32)
            z2 = z * z
            th = jnp.tanh(GELU_A * (z + GELU_B * z2 * z))
            ga[n, rows, :] = (0.5 * z * (1.0 + th)).astype(BF16)
            slope = 0.5 * (1.0 + th) + 0.5 * z * (1.0 - th * th) * (GELU_A * (1.0 + 3.0 * GELU_B * z2))
            dgl = mm(dy[rows, :], w2, 1, 1).astype(BF16).astype(F32)
            dz = (dgl * slope).astype(BF16)
            dza[n, rows, :] = dz
            acc[rows, :] += mm(dz, w1t)
        dwa[n] = mm(ga[n], dy[...], 0, 0)

        @pl.when(other == 1)
        def _():
            pair_copy(0, slot).start()

    ring_begin(0)

    vec[...] = jnp.zeros_like(vec)
    for r in range(4):
        rows = slice(r * 128, r * 128 + 128)
        dh2 = acc[rows, :].astype(BF16).astype(F32)
        x_hat, inv_std = norm_stats(x1[rows, :].astype(F32))
        dy_r = dy[rows, :].astype(F32)
        dx1_r = (dy_r + norm_back(dh2, x_hat, inv_std, gain2)).astype(BF16)
        dx1[rows, :] = dx1_r
        vec[2:3, :] += jnp.sum(dx1_r.astype(F32), axis=0, keepdims=True)
        vec[3:4, :] += jnp.sum(dh2 * x_hat, axis=0, keepdims=True)
        vec[4:5, :] += jnp.sum(dh2, axis=0, keepdims=True)
        vec[5:6, :] += jnp.sum(dy_r, axis=0, keepdims=True)

    def do_copy(n, st):
        target = handler(n, st)
        hi = 0 if target == n else 1
        return rc(do_send.at[m64(n), m256(st)], do_all.at[hi, :, m256(me)], do_ss.at[n, st], do_rs.at[hi, me], target)

    for r in range(2):
        rows = slice(r * 256, r * 256 + 256)
        do_send[rows, :] = mm(wo_all[rows, :], dx1[...], 1, 1).astype(BF16)
    for n in range(n_dev):
        for st in range(2):
            @pl.when(me != handler(n, st))
            def _():
                do_copy(n, st).start()

            @pl.when(me == handler(n, st))
            def _():
                do_all[0 if handler(n, st) == n else 1, :, m256(me)] = do_send[m64(n), m256(st)]

    @pl.loop(0, n_dev)
    def _(i):
        t, other = lax.div(i, 2), 1 - lax.rem(i, 2)
        slot = lax.rem(chip + 2 + t, chips)
        n = 2 * slot + core + other * (1 - 2 * core)
        dwb[n, 0:256, :] = mm(dza[n], h2[...], 0, 0)
        dwb[n, 256:320, :] = mm(o_all[m64(n), :], dx1[...])
        dwb[n, 320:336, 0:256] = jnp.broadcast_to(jnp.sum(dza[n].astype(F32), axis=0, keepdims=True), (16, 256))
        dwb[n, 320:336, 256:512] = jnp.zeros((16, 256), F32)

        @pl.when(other == 1)
        def _():
            pair_copy(1, slot).start()

    ring_turn(0)
    ring_begin(1)

    for j in range(n_dev):
        for hi in range(2):
            @pl.when(me != j)
            def _():
                rc(do_send.at[m64(0), m256(0)], do_all.at[hi, :, m256(j)], do_ss.at[0, 0], do_rs.at[hi, j], PT).wait_recv()
            do_t = do_all[hi, :, m256(j)].astype(F32)
            do_s[hi, m256(j), :] = do_t.T.astype(BF16)
            delta[hi, :, m256(j)] = jnp.sum(do_t * o_own[hi, :, m256(j)].astype(F32), axis=0, keepdims=True)
    dwq[...] = jnp.zeros_like(dwq)

    def dwq_copy():
        return rc(dwq.at[1], dwq_r, wq_ss.at[1], wq_rs.at[1], mate)

    def dh_pair_copy(kb):
        return rc(dh_send.at[kb], dh_pair.at[kb // 2], dhp_ss.at[kb // 2], dhp_rs.at[kb // 2], PT)

    def dh_copy(kb):
        return rc(dh_send.at[kb], dh_all.at[chip], dh_ss.at[kb // 2], dh_rs.at[chip], kb)

    def dh_finish(kb):
        @pl.when(core == kb % 2)
        def _():
            dh_pair_copy(kb).wait_recv()
            total = (dh_send[kb].astype(F32) + dh_pair[kb // 2].astype(F32)).astype(BF16)
            dh_send[kb] = total

            @pl.when(me != kb)
            def _():
                dh_copy(kb).start()

            @pl.when(me == kb)
            def _():
                dh_all[chip] = total

    @pl.loop(0, 2)
    def _(i):
        hi = 1 - i

        @pl.when(i == 1)
        def _():
            dwq_copy().start()

        for kb in range(n_dev):
            rows = m256(kb)
            k_b, v_b, kt_b = k_s[hi, rows, :], v_s[hi, rows, :], qkvt[hi, 64:128, rows]
            dk = jnp.zeros((256, 64), F32)
            dv = jnp.zeros((256, 64), F32)
            for qb in range(kb, n_dev):
                cols = m256(qb)
                p = jnp.exp2(mm(k_b, qkvt[hi, 0:64, cols]) * s_fac - lse[hi, :, cols])
                if qb == kb:
                    p = jnp.where(keep, p, 0.0)
                dp = mm(v_b, do_all[hi, :, cols]).astype(BF16).astype(F32)
                ds = (p * (dp - delta[hi, :, cols]) * attn_scale).astype(BF16)
                dv = dv + mm(p.astype(BF16), do_s[hi, cols, :])
                dk = dk + mm(ds, q_s[hi, cols, :])
                dq = mm(kt_b, ds)
                if kb == 0:
                    dqt[:, cols] = dq
                else:
                    dqt[:, cols] += dq
            dqkvt[hi, 0:64, rows] = dqt[:, rows].astype(BF16)
            dqkvt[hi, 64:192, rows] = jnp.concatenate([dk, dv], axis=1).T.astype(BF16)
            blk = dqkvt[hi, :, rows]
            dwq[hi, 0:192, :] += mm(blk, h1[rows, :])
            dwq[hi, 192:200, 0:192] += mm(jnp.ones((8, 256), BF16), blk, 1, 1)

            @pl.when(i == 1)
            def _():
                dh = mm(dqkvt[0, :, rows], wqp[0, 0:192, :], 0, 0) + mm(dqkvt[1, :, rows], wqp[1, 0:192, :], 0, 0)
                dh_send[kb] = dh.astype(BF16)

                @pl.when(core != kb % 2)
                def _():
                    dh_pair_copy(kb).start()

                if kb > 0:
                    dh_finish(kb - 1)

            if kb == 2:
                @pl.when(i == 0)
                def _():
                    ring_turn(1)

    dh_finish(n_dev - 1)

    for g in range(2):
        ring_copy(g, 2).wait_recv()
        ring_copy(g, 3).wait_recv()
    dwd_out[...] = dwa[me] + ra_l[...] + ra_r[...]
    dwu_out[...] = (dwb[me, 0:256, :] + rb_l[0:256, :] + rb_r[0:256, :]).T
    dwo_out[...] = dwb[me, 256:320, :] + rb_l[256:320, :] + rb_r[256:320, :]
    dbu_out[...] = dwb[me, 320:328, 0:256] + rb_l[320:328, 0:256] + rb_r[320:328, 0:256]

    acc[...] = jnp.zeros_like(acc)

    @pl.loop(0, n_dev)
    def _(n):
        for r in range(2):
            rows = slice(r * 256, r * 256 + 256)
            acc[rows, :] += mm(ga[n, rows, :], wp[n, 0:256, :])

    y_out[...] = (x1[...].astype(F32) + acc[...] + vector(bd)).astype(BF16)

    for t in range(chips):
        @pl.when(chip != t)
        def _():
            rc(dh_send.at[0], dh_all.at[t], dh_ss.at[0], dh_rs.at[t], PT).wait_recv()

    for r in range(4):
        rows = slice(r * 128, r * 128 + 128)
        half = slice((r % 2) * 128, (r % 2) * 128 + 128)
        first = (r // 2) * (chips // 2)
        dh1 = (dh_all[first, half, :].astype(F32) + dh_all[first + 1, half, :].astype(F32)).astype(BF16).astype(F32)
        x_hat, inv_std = norm_stats(x[rows, :].astype(F32))
        dx_out[rows, :] = (dx1[rows, :].astype(F32) + norm_back(dh1, x_hat, inv_std, gain1)).astype(BF16)
        vec[0:1, :] += jnp.sum(dh1 * x_hat, axis=0, keepdims=True)
        vec[1:2, :] += jnp.sum(dh1, axis=0, keepdims=True)

    def vec_copy(j):
        return rc(vec, vec_all.at[me], v_ss.at[j], v_rs.at[me], j)

    for j in range(n_dev):
        @pl.when(me != j)
        def _():
            vec_copy(j).start()
    vec_all[me] = vec[...]
    dwq_copy().wait_recv()
    dwqkv_out[...] = dwq[0] + dwq_r[...]
    for j in range(n_dev):
        @pl.when(me != j)
        def _():
            rc(vec, vec_all.at[j], v_ss.at[0], v_rs.at[j], PT).wait_recv()
    total = vec_all[0]
    for j in range(1, n_dev):
        total = total + vec_all[j]
    vec_out[...] = total

    wq_copy().wait_send()
    dwq_copy().wait_send()
    for t in range(chips):
        h1_pair(t, False).wait_send()

        @pl.when(chip != t)
        def _():
            h1_send(t).wait_send()
        for g in range(2):
            pair_copy(g, t).wait_send()
    for a in range(2):
        for ch in range(9):
            ag_copy(a, ch, False).wait_send()
    for g in range(2):
        for step in range(4):
            ring_copy(g, step).wait_send()
    for j in range(n_dev):
        @pl.when(me != j)
        def _():
            vec_copy(j).wait_send()
            for hi in range(2):
                o_copy(hi, j).wait_send()

        for st in range(2):
            @pl.when(me != handler(j, st))
            def _():
                do_copy(j, st).wait_send()

        @pl.when(core != j % 2)
        def _():
            dh_pair_copy(j).wait_send()

        @pl.when((core == j % 2) & (me != j))
        def _():
            dh_copy(j).wait_send()


def finish_kernel(y, dx, vec, dwqkv, dwo, dwu, dbu, dwd, y_o, dx_o, v0, v1, dwqkv_o, dbqkv_o, dwo_o, v2, v3, v4, dwu_o, dbu_o, dwd_o, v5):
    y_o[...] = y[...]
    dx_o[...] = dx[...]
    for i, ref in enumerate((v0, v1, v2, v3, v4, v5)):
        ref[...] = vec[i:i + 1, :].reshape(ref.shape)
    dwqkv_o[...] = dwqkv[0:192, :]
    for c in range(3):
        dbqkv_o[c] = dwqkv[192:193, c * 64:(c + 1) * 64]
    dwo_o[...] = dwo[...]
    dwu_o[...] = dwu[...]
    dbu_o[...] = dbu[0:1, :].reshape(dbu_o.shape)
    dwd_o[...] = dwd[...]


def solution(mesh):
    n_dev = mesh.shape["tp"]

    def device_step(hidden, grad_out, ln1_gain, ln1_bias, w_qkv, b_qkv, w_out, b_out, ln2_gain, ln2_bias, w_up, b_up, w_down, b_down):
        batch, tokens, d = hidden.shape
        rows = batch * tokens
        head = w_qkv.shape[-1]
        seq = tokens * n_dev
        ff = w_up.shape[1]
        chips = n_dev // 2
        attn_scale = head ** -0.5
        sds = jax.ShapeDtypeStruct
        vm = pltpu.VMEM

        def dma(*shape):
            return pltpu.SemaphoreType.DMA(shape)

        vspec = pl.BlockSpec(memory_space=pltpu.VMEM)
        outs = pl.pallas_call(
            lambda *refs: layer_kernel(n_dev, attn_scale, *refs),
            out_shape=(sds((rows, d), BF16), sds((rows, d), BF16), sds((8, d), F32), sds((200, d), F32),
                       sds((head, d), F32), sds((d, ff), F32), sds((8, ff), F32), sds((ff, d), F32)),
            in_specs=[vspec] * 14,
            out_specs=tuple([vspec] * 8),
            scratch_shapes=[
                vm((2, tokens, d), BF16), vm((seq, d), BF16), vm((n_dev, WO_ROWS, d), BF16), vm((n_dev, W_ROWS, d), BF16),
                vm((2, 208, d), BF16), vm((d, 512), BF16),
                vm((2, seq, head), BF16), vm((2, seq, head), BF16), vm((2, seq, head), BF16), vm((2, 3 * head, seq), BF16),
                vm((16, 256, 256), F32), vm((2, 1, seq), F32), vm((2, head, seq), BF16), vm((n_dev * head, rows), BF16),
                vm((n_dev * head, d), BF16), vm((rows, d), BF16), vm((rows, d), BF16),
                vm((n_dev, rows, ff), BF16), vm((n_dev, rows, ff), BF16), vm((rows, d), F32), vm((rows, d), BF16),
                vm((n_dev * head, rows), BF16), vm((2, head, seq), BF16), vm((2, seq, head), BF16),
                vm((2, 1, seq), F32), vm((head, seq), F32), vm((2, 3 * head, seq), BF16),
                vm((n_dev, tokens, d), BF16), vm((chips, tokens, d), BF16), vm((chips, tokens, d), BF16),
                vm((2, 200, d), F32), vm((200, d), F32),
                vm((n_dev, ff, d), F32), vm((n_dev, GB_ROWS, d), F32), vm((chips, ff, d), F32), vm((chips, GB_ROWS, d), F32),
                vm((ff // 2, d), F32), vm((ff // 2, d), F32), vm((ff, d), F32), vm((ff, d), F32),
                vm((GB_ROWS // 2, d), F32), vm((GB_ROWS // 2, d), F32), vm((GB_ROWS, d), F32), vm((GB_ROWS, d), F32),
                vm((8, d), F32), vm((n_dev, 8, d), F32),
                dma(chips), dma(chips), dma(chips), dma(chips), dma(2), dma(2), dma(2, 9), dma(2, 9), dma(2, n_dev), dma(2, n_dev),
                dma(n_dev, 2), dma(2, n_dev), dma(chips), dma(chips), dma(chips), dma(chips),
                dma(2, chips), dma(2, chips), dma(2, 4), dma(2, 4), dma(n_dev), dma(n_dev),
            ],
            compiler_params=pltpu.CompilerParams(collective_id=0, has_side_effects=True, vmem_limit_bytes=67043328),
            name="layer",
        )(hidden.reshape(rows, d), grad_out.reshape(rows, d), ln1_gain, ln1_bias, b_out, ln2_gain, ln2_bias, b_down,
          w_qkv.transpose(1, 2, 3, 0).reshape(3 * head, d), b_qkv, w_out.reshape(head, d), w_up, b_up, w_down)
        v1d = sds((d,), F32)
        y, dx, v0, v1, dwqkv_t, dbqkv, dwo, v2, v3, v4, dwu, dbu, dwd, v5 = pl.pallas_call(
            finish_kernel,
            out_shape=(sds((rows, d), BF16), sds((rows, d), BF16), v1d, v1d, sds((3 * head, d), F32), sds((3, 1, head), F32),
                       sds((head, d), F32), v1d, v1d, v1d, sds((d, ff), F32), sds((ff,), F32), sds((ff, d), F32), v1d),
            in_specs=[vspec] * 8,
            out_specs=tuple([vspec] * 14),
            name="finish",
        )(*outs)
        return (y.reshape(hidden.shape), dx.reshape(hidden.shape), v0, v1, dwqkv_t.reshape(3, 1, head, d).transpose(3, 0, 1, 2),
                dbqkv, dwo.reshape(w_out.shape), v2, v3, v4, dwu, dbu, dwd, v5)

    act_spec = P("dp", "tp", None)
    vec_spec = P(None)
    group_vec = P("dp")
    in_specs = (act_spec, act_spec, vec_spec, vec_spec, P(None, None, "tp", None), P(None, "tp", None), P("tp", None, None), vec_spec, vec_spec, vec_spec, P(None, "tp"), P("tp"), P("tp", None), vec_spec)
    out_specs = (act_spec, act_spec, group_vec, group_vec, P("dp", None, "tp", None), P("dp", "tp", None), P(("dp", "tp"), None, None), group_vec, group_vec, group_vec, P("dp", "tp"), P(("dp", "tp")), P(("dp", "tp"), None), group_vec)
    return jax.shard_map(device_step, mesh=mesh, in_specs=in_specs, out_specs=out_specs, check_vma=False)
```

time: 462 us -> 148 us (0.32)
  the two profiles are of different devices: /device:TPU:112 before, /device:TPU:113 now
where the time goes in v2:
time: 148 us
  Pallas kernels  146 us (99%)
    pallas_call x1, Pallas kernels, device_step(): pl.pallas_call(lambda *refs: layer_kernel(n_dev, attn_scale, *refs), out_...  143 us
    pallas_call x1, Pallas kernels, device_step(): pl.pallas_call(finish_kernel, out_shape=(sds((rows, d), BF16), sds((rows,...  3.3 us

profile of v2, /device:TPU:113, one launch (start us, length us, event | category | flops | bytes accessed | tf_op | source)
XLA Modules:
  0.0 147.9 jit_solution(14452088164721659659)
XLA Ops:
  0.6 0.0 copy-start
  0.7 0.7 copy-done
  1.3 0.6 copy.28.refs_9_
  1.9 142.5 %layer.1 = (bf16[512,512]{1,0:T(8,128)(2,1)}, bf16[512,512]{1,0:T(8,128)(2,1)}, f32[8,512]{1,0:T(8,128)}, f32[200,512]{1,0:T(8,128)}, f32[64,512]{1,0:T(8,128)},...) custom-call(bf16[512,512]{1,0:T(8,128)(2,1)} %bitcast.14, bf16[512,512]{1,0:T(8,128)(2,1)} %bitcast.15, ...), custom_call_target="tpu_custom_call" | custom-call | tf_op jit(solution)/shard_map/layer/pallas_call | solution.py:588
  144.4 3.3 %finish.1 = (bf16[512,512]{1,0:T(8,128)(2,1)}, bf16[512,512]{1,0:T(8,128)(2,1)}, f32[512]{0:T(512)}, f32[512]{0:T(512)}, f32[192,512]{1,0:T(8,128)}, /*index=5*/...) custom-call(bf16[512,512]{1,0:T(8,128)(2,1)} %get-tuple-element.36.y, ...), custom_call_target="tpu_custom_call" | custom-call | tf_op jit(solution)/shard_map/finish/pallas_call | solution.py:618
Async XLA Ops:
  0.6 0.7 copy-start

commit v3 on v2

--- a/solution.py
+++ b/solution.py
@@ -13,8 +13,8 @@
 GELU_A = 0.7978845608028654
 GELU_B = 0.044715
 
-W_ROWS, WO_ROWS = 512, 80
-GB_ROWS = 336
+WO_ROWS = 80
+G_ROWS = 528
 
 
 def mm(lhs, rhs, lc=1, rc=0):
@@ -39,22 +39,23 @@
 def layer_kernel(n_dev, attn_scale,
                  x, dy, g1, s1, bo, g2, s2, bd, wqkv, bqkv, wo, wu, bu, wd,
                  y_out, dx_out, vec_out, dwqkv_out, dwo_out, dwu_out, dbu_out, dwd_out,
-                 h1own, h1, wob, wp, wqp, wq, q_s, k_s, v_s, qkvt, big, lse, o_own, o_all, wo_all, x1, h2, ga, dza, acc, dx1,
+                 h1own, h1, wob, wp, wqp, wq, q_s, k_s, v_s, qkvt, big, lse, o_own, o_all, wo_all, x1, hh, dyy, ga, dza, acc, dx1,
                  do_send, do_all, do_s, delta, dqt, dqkvt, dh_send, dh_pair, dh_all, dwq, dwq_r,
-                 dwa, dwb, pra, prb, ra_a, ra_b, ra_l, ra_r, rb_a, rb_b, rb_l, rb_r, vec, vec_all,
-                 hs_ss, hs_rs, hp_ss, hp_rs, wq_ss, wq_rs, ag_ss, ag_rs, o_ss, o_rs, do_ss, do_rs, dhp_ss, dhp_rs, dh_ss, dh_rs,
-                 pr_ss, pr_rs, rg_ss, rg_rs, v_ss, v_rs):
+                 dwp, prx, frx, dwop, dwo_pr, dwo_rx, vec, vec_all,
+                 hs_ss, hs_rs, hp_ss, hp_rs, wq_ss, wq_rs, wb_ss, wb_rs, o_ss, o_rs, do_ss, do_rs, dhp_ss, dhp_rs, dh_ss, dh_rs,
+                 wp_ss, wp_rs, mt_ss, mt_rs, pr_ss, pr_rs, fr_ss, fr_rs, op_ss, op_rs, ox_ss, ox_rs, v_ss, v_rs):
     me = lax.axis_index("tp")
     chips = n_dev // 2
     chip, core = lax.div(me, 2), lax.rem(me, 2)
     seq = lax.div(chip, chips // 2)
     mate = 2 * (chips - 1 - chip) + core
+    side = chip + 1 - 2 * lax.rem(chip, 2)
+    flank, across = 2 * side + core, 2 * (chips - 1 - side) + core
 
     def dev(shift, other):
         return 2 * lax.rem(chip + shift + chips, chips) + (1 - core if other else core)
 
-    L, R, O, PT = dev(-1, False), dev(1, False), dev(2, False), dev(0, True)
-    PL, PR, PO = dev(-1, True), dev(1, True), dev(2, True)
+    PT = dev(0, True)
 
     def handler(n, st):
         return n if (n // 2) // (chips // 2) == st else 2 * (chips - 1 - n // 2) + n % 2
@@ -68,27 +69,6 @@
 
     def m64(i):
         return pl.ds(i * 64, 64) if isinstance(i, int) else pl.ds(pl.multiple_of(i * 64, 64), 64)
-
-    plan = ((me, "F", R, L), (me, "F", L, R), (me, "F", PT, PT), (L, "A", R, O), (R, "B", L, O),
-            (L, "F", PT, PL), (R, "F", PT, PR), (O, "A", PT, PO), (O, "B", PT, PO))
-
-    def view(a, owner, part):
-        cut, rows = ((48, WO_ROWS), (256, W_ROWS))[a]
-        off, size = {"F": (0, rows), "A": (0, cut), "B": (cut, rows - cut)}[part]
-        return (wob, wp)[a].at[owner, pl.ds(off, size), :]
-
-    def ag_copy(a, ch, received):
-        own, part, target, got = plan[ch]
-        v = view(a, got if received else own, part)
-        return rc(v, v, ag_ss.at[a, ch], ag_rs.at[a, ch], target)
-
-    def ag_start(a, *chs):
-        for ch in chs:
-            ag_copy(a, ch, False).start()
-
-    def ag_wait(a, *chs):
-        for ch in chs:
-            ag_copy(a, ch, True).wait_recv()
 
     barrier = pltpu.get_barrier_semaphore()
     for i in range(n_dev):
@@ -107,11 +87,12 @@
     bq_row = jnp.concatenate([bqkv[c].astype(F32) for c in range(3)] + [jnp.zeros((1, 320), F32)], axis=1)
     wqp[0, 192:208, :] = jnp.broadcast_to(bq_row, (16, 512)).astype(BF16)
 
-    def h1_send(t):
-        return rc(h1own.at[t // (chips // 2)], h1.at[m256(me), :], hs_ss.at[t], hs_rs.at[chip], 2 * t + core)
-
-    def h1_recv(src):
-        return rc(h1own.at[0], h1.at[m256(2 * src + core), :], hs_ss.at[0], hs_rs.at[src], PT)
+    def h1_copy(step):
+        src, row, target = ((h1own.at[1 - seq], me, mate), (h1own.at[seq], me, flank), (h1.at[m256(mate), :], mate, flank))[step]
+        return rc(src, h1.at[m256(row), :], hs_ss.at[step], hs_rs.at[step], target)
+
+    def h1_recv(step, src):
+        return rc(h1own.at[0], h1.at[m256(2 * src + core), :], hs_ss.at[0], hs_rs.at[step], PT)
 
     def h1_pair(src, received):
         rows = m256(2 * src + (1 - core if received else core))
@@ -121,11 +102,8 @@
         return rc(wqp.at[0], wqp.at[1], wq_ss.at[0], wq_rs.at[0], mate)
 
     pl.semaphore_wait(barrier, n_dev - 1)
-    wq_copy().start()
-    for t in range(chips):
-        @pl.when(chip != t)
-        def _():
-            h1_send(t).start()
+    h1_copy(0).start()
+    h1_copy(1).start()
     h1_pair(chip, False).start()
 
     wob[me, 0:64, :] = wo[...]
@@ -133,41 +111,94 @@
     wob[me, 64:80, 256:512] = jnp.zeros((16, 256), BF16)
     wp[me, 0:256, :] = wd[...]
     wp[me, 256:512, :] = wu[...].astype(F32).T.astype(BF16)
+    dyy[0:512, :] = dy[...]
+
+    def twin(d):
+        return d + 1 - 2 * core
+
+    w_plan = ((me, PT, PT, 0, 512), (me, mate, mate, 0, 256), (me, mate, mate, 256, 256), (me, flank, flank, 0, 512),
+              (mate, flank, across, 0, 256), (mate, flank, across, 256, 256),
+              (flank, PT, twin(flank), 0, 512), (mate, PT, twin(mate), 0, 512), (across, PT, twin(across), 0, 512))
+
+    def w_copy(step, received=False):
+        own, target, got, off, size = w_plan[step]
+        v = wp.at[got if received else own, pl.ds(off, size), :]
+        return rc(v, v, wp_ss.at[step], wp_rs.at[step], target)
+
+    def w_wait(*steps):
+        for step in steps:
+            w_copy(step, True).wait_recv()
+
+    def w_start(*steps):
+        for step in steps:
+            w_copy(step).start()
+
+    o_plan = ((me, PT, PT), (me, mate, mate), (me, flank, flank), (mate, flank, across),
+              (flank, PT, twin(flank)), (mate, PT, twin(mate)), (across, PT, twin(across)))
+
+    def wo_all_copy(step, received=False):
+        own, target, got = o_plan[step]
+        v = wob.at[got if received else own]
+        return rc(v, v, wb_ss.at[step], wb_rs.at[step], target)
+
+    def wo_wait(*steps):
+        for step in steps:
+            wo_all_copy(step, True).wait_recv()
+
+    def wo_start(*steps):
+        for step in steps:
+            wo_all_copy(step).start()
+
+    wo_start(0)
+
+    def mate_copy(step):
+        src, dst = ((hh.at[0:256], hh.at[512:768]), (hh.at[256:512], hh.at[768:1024]), (dyy.at[0:512], dyy.at[512:1024]))[step]
+        return rc(src, dst, mt_ss.at[step], mt_rs.at[step], mate)
+
+    w_start(0)
 
     def natural(hi):
         full = jnp.concatenate([wqp[hi, 0:192, :].astype(F32), jnp.zeros((64, 512), F32)], axis=0)
         wq[:, hi * 256:(hi + 1) * 256] = full.T.astype(BF16)
 
     natural(0)
-    wq_copy().wait_recv()
-    natural(1)
-    bias_qkv = jnp.concatenate([wqp[hi, 192:208, 0:256].astype(F32)[0:1, :] for hi in range(2)], axis=1)
-
-    def project(owner):
+
+    def project(owner, hi):
         rows = m256(owner)
-        full = (mm(h1[rows, :], wq[...]) + bias_qkv).astype(BF16).astype(F32)
-        for hi in range(2):
-            part = full[:, hi * 256:(hi + 1) * 256]
-            q_s[hi, rows, :] = part[:, 0:64].astype(BF16)
-            k_s[hi, rows, :] = part[:, 64:128].astype(BF16)
-            v_s[hi, rows, :] = part[:, 128:192].astype(BF16)
-            qkvt[hi, :, rows] = part.T[:192, :].astype(BF16)
+        bias = wqp[hi, 192:208, 0:256].astype(F32)[0:1, :]
+        part = (mm(h1[rows, :], wq[:, hi * 256:(hi + 1) * 256]) + bias).astype(BF16).astype(F32)
+        q_s[hi, rows, :] = part[:, 0:64].astype(BF16)
+        k_s[hi, rows, :] = part[:, 64:128].astype(BF16)
+        v_s[hi, rows, :] = part[:, 128:192].astype(BF16)
+        qkvt[hi, :, rows] = part.T[:192, :].astype(BF16)
+
+    def near(t):
+        base = chip + lax.div(t, 2) * (side - chip)
+        return base + lax.rem(t, 2) * (chips - 1 - 2 * base)
 
     @pl.loop(0, chips)
     def _(t):
-        src = lax.rem(chip + t + lax.div(t, 2) - 2 * lax.div(t, 3), chips)
+        src = near(t)
+
+        @pl.when(t == 2)
+        def _():
+            wq_copy().start()
+            wo_start(1, 2)
+            w_start(1, 2, 3)
 
         @pl.when(t > 0)
         def _():
-            h1_recv(src).wait_recv()
+            h1_recv(t - 1, src).wait_recv()
             h1_pair(src, False).start()
 
-        project(2 * src + core)
+        @pl.when(t == 1)
+        def _():
+            h1_copy(2).start()
+
+        project(2 * src + core, 0)
         h1_pair(src, True).wait_recv()
-        project(2 * src + 1 - core)
-
-    for a in range(2):
-        ag_start(a, 0, 1, 2)
+        project(2 * src + 1 - core, 0)
+
 
     s_fac = attn_scale * LOG2E
     keep = lax.broadcasted_iota(jnp.int32, (256, 256), 0) <= lax.broadcasted_iota(jnp.int32, (256, 256), 1)
@@ -215,19 +246,37 @@
     def _(hi):
         @pl.when(hi == 1)
         def _():
-            ag_wait(0, 0, 1, 2)
-            ag_start(0, 3, 4, 5, 6)
+            wq_copy().wait_recv()
+            natural(1)
+
+            @pl.loop(0, n_dev)
+            def _(owner):
+                project(owner, 1)
 
         for j in range(n_dev):
             attend(hi, j)
-
-    ag_wait(1, 0)
-    ag_start(1, 3, 5)
-    ag_wait(1, 1)
-    ag_start(1, 4, 6)
-    ag_wait(0, 3, 4)
-    ag_start(0, 7, 8)
-    ag_wait(0, 5, 6, 7, 8)
+            if j == 4:
+                @pl.when(hi == 1)
+                def _():
+                    w_wait(1)
+                    w_start(4)
+            if j == 2:
+                @pl.when(hi == 1)
+                def _():
+                    wo_wait(1)
+                    wo_start(3, 5)
+            if j == 6:
+                @pl.when(hi == 1)
+                def _():
+                    wo_wait(2, 3)
+                    wo_start(4, 6)
+
+    mate_copy(2).start()
+    w_wait(2)
+    w_start(5)
+    w_wait(3)
+    w_start(6, 7)
+    wo_wait(0, 4, 5, 6)
     for n in range(n_dev):
         wo_all[n * 64:(n + 1) * 64, :] = wob[n, 0:64, :]
     for st in range(2):
@@ -244,91 +293,46 @@
         x1_r = (x[rows, :].astype(F32) + attn + bias_o).astype(BF16)
         x1[rows, :] = x1_r
         x_hat, _ = norm_stats(x1_r.astype(F32))
-        h2[rows, :] = (x_hat * gain2 + shift2).astype(BF16)
+        hh[rows, :] = (x_hat * gain2 + shift2).astype(BF16)
+        if r % 2 == 1:
+            mate_copy(r // 2).start()
+
+    def mlp(n, rows):
+        w2 = wp[n, 0:256, :]
+        w1t = wp[n, 256:512, :]
+        bias_u = wob[n, 64:80, 0:256].astype(F32)[0:1, :]
+        z = (mm(hh[rows, :], w1t, 1, 1) + bias_u).astype(BF16).astype(F32)
+        z2 = z * z
+        th = jnp.tanh(GELU_A * (z + GELU_B * z2 * z))
+        g = (0.5 * z * (1.0 + th)).astype(BF16)
+        slope = 0.5 * (1.0 + th) + 0.5 * z * (1.0 - th * th) * (GELU_A * (1.0 + 3.0 * GELU_B * z2))
+        dgl = mm(dyy[rows, :], w2, 1, 1).astype(BF16).astype(F32)
+        dz = (dgl * slope).astype(BF16)
+        ga[n, rows, :] = g
+        dza[n, rows, :] = dz
+        return dz, w1t
+
     acc[...] = jnp.zeros_like(acc)
-
-    packs = ((dwa, pra, ra_a, ra_b, ra_l, ra_r, 128), (dwb, prb, rb_a, rb_b, rb_l, rb_r, GB_ROWS // 2))
-
-    def pair_copy(g, slot):
-        return rc(packs[g][0].at[2 * slot + 1 - core], packs[g][1].at[slot], pr_ss.at[g, slot], pr_rs.at[g, slot], PT)
-
-    def pair_add(g, slot):
-        pair_copy(g, slot).wait_recv()
-        packs[g][0][2 * slot + core] += packs[g][1][slot]
-
-    def ring_copy(g, step):
-        pack, _, r_a, r_b, r_l, r_r, half = packs[g]
-        top, low = pl.ds(0, half), pl.ds(half, half)
-        src, dst, target = (
-            (pack.at[O, top, :], r_a, R), (pack.at[O, low, :], r_b, L), (pack.at[R], r_l, R), (pack.at[L], r_r, L))[step]
-        return rc(src, dst, rg_ss.at[g, step], rg_rs.at[g, step], target)
-
-    def ring_begin(g):
-        pair_add(g, lax.rem(chip + 2, chips))
-        ring_copy(g, 0).start()
-        ring_copy(g, 1).start()
-        for shift in (1, 3, 0):
-            pair_add(g, lax.rem(chip + shift, chips))
-
-    def ring_turn(g):
-        pack, _, r_a, r_b, _, _, half = packs[g]
-        ring_copy(g, 0).wait_recv()
-        pack[R, 0:half, :] += r_a[...]
-        ring_copy(g, 2).start()
-        ring_copy(g, 1).wait_recv()
-        pack[L, half:2 * half, :] += r_b[...]
-        ring_copy(g, 3).start()
 
     @pl.loop(0, n_dev)
     def _(i):
         t, other = lax.div(i, 2), lax.rem(i, 2)
-        slot = lax.rem(chip + t + lax.div(t, 2) - 2 * lax.div(t, 3), chips)
-        n = 2 * slot + core + other * (1 - 2 * core)
-
-        @pl.when(i == 1)
-        def _():
-            ag_wait(1, 2)
-
-        @pl.when(i == 3)
-        def _():
-            ag_wait(1, 6)
-
-        @pl.when(i == 5)
-        def _():
-            ag_wait(1, 5)
+        near_chip = chip + lax.rem(t, 2) * (side - chip)
+        n = 2 * (near_chip + lax.div(t, 2) * (chips - 1 - 2 * near_chip)) + core + other * (1 - 2 * core)
+        for step, at in ((0, 1), (6, 3), (7, 5), (8, 7)):
+            @pl.when(i == at)
+            def _():
+                w_wait(step)
 
         @pl.when(i == 6)
         def _():
-            ag_wait(1, 3)
-            ag_start(1, 7)
-            ag_wait(1, 4)
-            ag_start(1, 8)
-
-        @pl.when(i == 7)
-        def _():
-            ag_wait(1, 7, 8)
-
-        w2 = wp[n, 0:256, :]
-        w1t = wp[n, 256:512, :]
-        bias_u = wob[n, 64:80, 0:256].astype(F32)[0:1, :]
+            w_wait(4, 5)
+            w_start(8)
+
         for r in range(2):
             rows = slice(r * 256, r * 256 + 256)
-            z = (mm(h2[rows, :], w1t, 1, 1) + bias_u).astype(BF16).astype(F32)
-            z2 = z * z
-            th = jnp.tanh(GELU_A * (z + GELU_B * z2 * z))
-            ga[n, rows, :] = (0.5 * z * (1.0 + th)).astype(BF16)
-            slope = 0.5 * (1.0 + th) + 0.5 * z * (1.0 - th * th) * (GELU_A * (1.0 + 3.0 * GELU_B * z2))
-            dgl = mm(dy[rows, :], w2, 1, 1).astype(BF16).astype(F32)
-            dz = (dgl * slope).astype(BF16)
-            dza[n, rows, :] = dz
+            dz, w1t = mlp(n, rows)
             acc[rows, :] += mm(dz, w1t)
-        dwa[n] = mm(ga[n], dy[...], 0, 0)
-
-        @pl.when(other == 1)
-        def _():
-            pair_copy(0, slot).start()
-
-    ring_begin(0)
 
     vec[...] = jnp.zeros_like(vec)
     for r in range(4):
@@ -361,22 +365,81 @@
             def _():
                 do_all[0 if handler(n, st) == n else 1, :, m256(me)] = do_send[m64(n), m256(st)]
 
+    def wo_pair_copy(slot):
+        return rc(dwop.at[2 * slot + 1 - core], dwo_pr.at[slot], op_ss.at[slot], op_rs.at[slot], PT)
+
+    def wo_copy(t):
+        return rc(dwop.at[2 * t + core], dwo_rx.at[chip], ox_ss.at[t], ox_rs.at[chip], 2 * t + core)
+
+    for n in range(n_dev):
+        dwop[n] = mm(o_all[m64(n), :], dx1[...])
+    for t in range(chips):
+        wo_pair_copy(t).start()
+
+    acc[...] = jnp.zeros_like(acc)
+
     @pl.loop(0, n_dev)
+    def _(n):
+        for r in range(2):
+            rows = slice(r * 256, r * 256 + 256)
+            acc[rows, :] += mm(ga[n, rows, :], wp[n, 0:256, :])
+
+    y_out[...] = (x1[...].astype(F32) + acc[...] + vector(bd)).astype(BF16)
+
+    def pair_copy(which):
+        return rc(dwp.at[2 * which], prx.at[which], pr_ss.at[which], pr_rs.at[which], PT)
+
+    def side_copy(step):
+        rows = pl.ds(step * (G_ROWS // 3), G_ROWS // 3)
+        return rc(dwp.at[1, rows], frx.at[rows], fr_ss.at[step], fr_rs.at[step], flank)
+
+    def pair_add(which):
+        pair_copy(which).wait_recv()
+        dwp[2 * which + 1] += prx[which]
+
+    for t in range(chips):
+        wo_pair_copy(t).wait_recv()
+        dwop[2 * t + core] += dwo_pr[t]
+
+    wo_copy(side).start()
+
+    def block(i):
+        which, own = lax.div(i, 2), lax.rem(i, 2)
+        return which, own, 2 * (side + which * (chip - side)) + (1 - core) + own * (2 * core - 1)
+
+    @pl.loop(0, 4)
     def _(i):
-        t, other = lax.div(i, 2), 1 - lax.rem(i, 2)
-        slot = lax.rem(chip + 2 + t, chips)
-        n = 2 * slot + core + other * (1 - 2 * core)
-        dwb[n, 0:256, :] = mm(dza[n], h2[...], 0, 0)
-        dwb[n, 256:320, :] = mm(o_all[m64(n), :], dx1[...])
-        dwb[n, 320:336, 0:256] = jnp.broadcast_to(jnp.sum(dza[n].astype(F32), axis=0, keepdims=True), (16, 256))
-        dwb[n, 320:336, 256:512] = jnp.zeros((16, 256), F32)
-
-        @pl.when(other == 1)
-        def _():
-            pair_copy(1, slot).start()
-
-    ring_turn(0)
-    ring_begin(1)
+        _, _, n = block(i)
+        own_rows = slice(0, 512)
+        dwp[i, 0:256, :] = mm(ga[n, own_rows, :], dyy[own_rows, :], 0, 0)
+        dwp[i, 256:512, :] = mm(dza[n, own_rows, :], hh[own_rows, :], 0, 0)
+        dwp[i, 512:528, 0:256] = jnp.broadcast_to(jnp.sum(dza[n, own_rows, :].astype(F32), axis=0, keepdims=True), (16, 256))
+        dwp[i, 512:528, 256:512] = jnp.zeros((16, 256), F32)
+
+    mate_copy(2).wait_recv()
+    for r in range(2):
+        mate_copy(r).wait_recv()
+        rows = slice(512 + r * 256, 768 + r * 256)
+
+        @pl.loop(0, 4)
+        def _(i):
+            which, own, n = block(i)
+            mlp(n, rows)
+            dwp[i, 0:256, :] += mm(ga[n, rows, :], dyy[rows, :], 0, 0)
+            dwp[i, 256:512, :] += mm(dza[n, rows, :], hh[rows, :], 0, 0)
+            dwp[i, 512:528, 0:256] += jnp.broadcast_to(jnp.sum(dza[n, rows, :].astype(F32), axis=0, keepdims=True), (16, 256))
+            if r == 1:
+                @pl.when(own == 0)
+                def _():
+                    pair_copy(which).start()
+
+                @pl.when(i == 2)
+                def _():
+                    pair_add(0)
+                    for step in range(3):
+                        side_copy(step).start()
+
+    pair_add(1)
 
     for j in range(n_dev):
         for hi in range(2):
@@ -386,6 +449,10 @@
             do_t = do_all[hi, :, m256(j)].astype(F32)
             do_s[hi, m256(j), :] = do_t.T.astype(BF16)
             delta[hi, :, m256(j)] = jnp.sum(do_t * o_own[hi, :, m256(j)].astype(F32), axis=0, keepdims=True)
+    for t in range(chips):
+        @pl.when((chip != t) & (side != t))
+        def _():
+            wo_copy(t).start()
     dwq[...] = jnp.zeros_like(dwq)
 
     def dwq_copy():
@@ -457,30 +524,20 @@
                 if kb > 0:
                     dh_finish(kb - 1)
 
-            if kb == 2:
-                @pl.when(i == 0)
-                def _():
-                    ring_turn(1)
 
     dh_finish(n_dev - 1)
 
-    for g in range(2):
-        ring_copy(g, 2).wait_recv()
-        ring_copy(g, 3).wait_recv()
-    dwd_out[...] = dwa[me] + ra_l[...] + ra_r[...]
-    dwu_out[...] = (dwb[me, 0:256, :] + rb_l[0:256, :] + rb_r[0:256, :]).T
-    dwo_out[...] = dwb[me, 256:320, :] + rb_l[256:320, :] + rb_r[256:320, :]
-    dbu_out[...] = dwb[me, 320:328, 0:256] + rb_l[320:328, 0:256] + rb_r[320:328, 0:256]
-
-    acc[...] = jnp.zeros_like(acc)
-
-    @pl.loop(0, n_dev)
-    def _(n):
-        for r in range(2):
-            rows = slice(r * 256, r * 256 + 256)
-            acc[rows, :] += mm(ga[n, rows, :], wp[n, 0:256, :])
-
-    y_out[...] = (x1[...].astype(F32) + acc[...] + vector(bd)).astype(BF16)
+    for step in range(3):
+        side_copy(step).wait_recv()
+    dwd_out[...] = dwp[3, 0:256, :] + frx[0:256, :]
+    dwu_out[...] = (dwp[3, 256:512, :] + frx[256:512, :]).T
+    dbu_out[...] = dwp[3, 512:520, 0:256] + frx[512:520, 0:256]
+    dwo_rx[chip] = dwop[me]
+    for t in range(chips):
+        @pl.when(chip != t)
+        def _():
+            rc(dwop.at[0], dwo_rx.at[t], ox_ss.at[0], ox_rs.at[t], PT).wait_recv()
+    dwo_out[...] = dwo_rx[0] + dwo_rx[1] + dwo_rx[2] + dwo_rx[3]
 
     for t in range(chips):
         @pl.when(chip != t)
@@ -523,15 +580,21 @@
 
         @pl.when(chip != t)
         def _():
-            h1_send(t).wait_send()
-        for g in range(2):
-            pair_copy(g, t).wait_send()
-    for a in range(2):
-        for ch in range(9):
-            ag_copy(a, ch, False).wait_send()
-    for g in range(2):
-        for step in range(4):
-            ring_copy(g, step).wait_send()
+            wo_copy(t).wait_send()
+
+        wo_pair_copy(t).wait_send()
+    for step in range(9):
+        w_copy(step).wait_send()
+    for step in range(7):
+        wo_all_copy(step).wait_send()
+    for step in range(3):
+        h1_copy(step).wait_send()
+    for step in range(3):
+        mate_copy(step).wait_send()
+    for which in range(2):
+        pair_copy(which).wait_send()
+    for step in range(3):
+        side_copy(step).wait_send()
     for j in range(n_dev):
         @pl.when(me != j)
         def _():
@@ -592,23 +655,22 @@
             in_specs=[vspec] * 14,
             out_specs=tuple([vspec] * 8),
             scratch_shapes=[
-                vm((2, tokens, d), BF16), vm((seq, d), BF16), vm((n_dev, WO_ROWS, d), BF16), vm((n_dev, W_ROWS, d), BF16),
+                vm((2, tokens, d), BF16), vm((seq, d), BF16), vm((n_dev, WO_ROWS, d), BF16), vm((n_dev, 2 * ff, d), BF16),
                 vm((2, 208, d), BF16), vm((d, 512), BF16),
                 vm((2, seq, head), BF16), vm((2, seq, head), BF16), vm((2, seq, head), BF16), vm((2, 3 * head, seq), BF16),
                 vm((16, 256, 256), F32), vm((2, 1, seq), F32), vm((2, head, seq), BF16), vm((n_dev * head, rows), BF16),
-                vm((n_dev * head, d), BF16), vm((rows, d), BF16), vm((rows, d), BF16),
-                vm((n_dev, rows, ff), BF16), vm((n_dev, rows, ff), BF16), vm((rows, d), F32), vm((rows, d), BF16),
+                vm((n_dev * head, d), BF16), vm((rows, d), BF16), vm((2 * rows, d), BF16), vm((2 * rows, d), BF16),
+                vm((n_dev, 2 * rows, ff), BF16), vm((n_dev, 2 * rows, ff), BF16), vm((rows, d), F32), vm((rows, d), BF16),
                 vm((n_dev * head, rows), BF16), vm((2, head, seq), BF16), vm((2, seq, head), BF16),
                 vm((2, 1, seq), F32), vm((head, seq), F32), vm((2, 3 * head, seq), BF16),
                 vm((n_dev, tokens, d), BF16), vm((chips, tokens, d), BF16), vm((chips, tokens, d), BF16),
                 vm((2, 200, d), F32), vm((200, d), F32),
-                vm((n_dev, ff, d), F32), vm((n_dev, GB_ROWS, d), F32), vm((chips, ff, d), F32), vm((chips, GB_ROWS, d), F32),
-                vm((ff // 2, d), F32), vm((ff // 2, d), F32), vm((ff, d), F32), vm((ff, d), F32),
-                vm((GB_ROWS // 2, d), F32), vm((GB_ROWS // 2, d), F32), vm((GB_ROWS, d), F32), vm((GB_ROWS, d), F32),
+                vm((4, G_ROWS, d), F32), vm((2, G_ROWS, d), F32), vm((G_ROWS, d), F32),
+                vm((n_dev, head, d), F32), vm((chips, head, d), F32), vm((chips, head, d), F32),
                 vm((8, d), F32), vm((n_dev, 8, d), F32),
-                dma(chips), dma(chips), dma(chips), dma(chips), dma(2), dma(2), dma(2, 9), dma(2, 9), dma(2, n_dev), dma(2, n_dev),
+                dma(chips), dma(chips), dma(chips), dma(chips), dma(2), dma(2), dma(7), dma(7), dma(2, n_dev), dma(2, n_dev),
                 dma(n_dev, 2), dma(2, n_dev), dma(chips), dma(chips), dma(chips), dma(chips),
-                dma(2, chips), dma(2, chips), dma(2, 4), dma(2, 4), dma(n_dev), dma(n_dev),
+                dma(9), dma(9), dma(3), dma(3), dma(2), dma(2), dma(3), dma(3), dma(chips), dma(chips), dma(chips), dma(chips), dma(n_dev), dma(n_dev),
             ],
             compiler_params=pltpu.CompilerParams(collective_id=0, has_side_effects=True, vmem_limit_bytes=67043328),
             name="layer",

time: 148 us -> 129 us (0.87)
  Pallas kernels: 146 us -> 126 us
    pallas_call x1, Pallas kernels: 143 us -> 123 us  [device_step(): pl.pallas_call(lambda *refs: layer_kernel(n_dev, attn_scale, *refs), out_...]
where the time goes in v3:
time: 129 us; the launch traced here: 128 us
  Pallas kernels  126 us (98%)
    pallas_call x1, Pallas kernels, device_step(): pl.pallas_call(lambda *refs: layer_kernel(n_dev, attn_scale, *refs), out_...  123 us
    pallas_call x1, Pallas kernels, device_step(): pl.pallas_call(finish_kernel, out_shape=(sds((rows, d), BF16), sds((rows,...  3.3 us

profile of v3, /device:TPU:113, one launch (start us, length us, event | category | flops | bytes accessed | tf_op | source)
XLA Modules:
  0.0 128.5 jit_solution(8512116239376668115)
XLA Ops:
  0.6 0.0 copy-start
  0.7 0.7 copy-done
  1.3 0.6 copy.28.refs_9_
  1.9 123.1 %layer.1 = (bf16[512,512]{1,0:T(8,128)(2,1)}, bf16[512,512]{1,0:T(8,128)(2,1)}, f32[8,512]{1,0:T(8,128)}, f32[200,512]{1,0:T(8,128)}, f32[64,512]{1,0:T(8,128)},...) custom-call(bf16[512,512]{1,0:T(8,128)(2,1)} %bitcast.14, bf16[512,512]{1,0:T(8,128)(2,1)} %bitcast.15, ...), custom_call_target="tpu_custom_call" | custom-call | tf_op jit(solution)/shard_map/layer/pallas_call | solution.py:651
  125.0 3.3 %finish.1 = (bf16[512,512]{1,0:T(8,128)(2,1)}, bf16[512,512]{1,0:T(8,128)(2,1)}, f32[512]{0:T(512)}, f32[512]{0:T(512)}, f32[192,512]{1,0:T(8,128)}, /*index=5*/...) custom-call(bf16[512,512]{1,0:T(8,128)(2,1)} %get-tuple-element.36.y, ...), custom_call_target="tpu_custom_call" | custom-call | tf_op jit(solution)/shard_map/finish/pallas_call | solution.py:680
Async XLA Ops:
  0.6 0.7 copy-start

commit v4 on v3

v4 whole, which is shorter than its diff:
```python
import jax
import jax.numpy as jnp
from jax import lax
from jax.experimental import pallas as pl
from jax.experimental.pallas import tpu as pltpu
from jax.sharding import PartitionSpec as P

LN_EPS = 1e-5
MESH = pl.DeviceIdType.MESH
F32 = jnp.float32
BF16 = jnp.bfloat16
LOG2E = 1.4426950408889634
GELU_A = 0.7978845608028654
GELU_AB = GELU_A * 0.044715

TOK = 256
WIDTH = 512
HEAD = 64
HALF = 128
QKV = 192
SUB = 8
TAIL = 320
WQ_ROWS = 208
PACK = 16
THREE = 3
DW_ROWS = 200
SEQ = 2048
FOUR = 4
WO_ROWS = 80
G_ROWS = 528


def mm(lhs, rhs, lc=1, rc=0):
    return lax.dot_general(lhs, rhs, (((lc,), (rc,)), ((), ())), preferred_element_type=F32)


def norm_stats(value):
    centered = value - jnp.mean(value, axis=-1, keepdims=True)
    inv_std = lax.rsqrt(jnp.mean(centered * centered, axis=-1, keepdims=True) + LN_EPS)
    return centered * inv_std, inv_std


def norm_back(grad, x_hat, inv_std, gain):
    scaled = grad * gain
    return inv_std * (scaled - jnp.mean(scaled, axis=-1, keepdims=True) - x_hat * jnp.mean(scaled * x_hat, axis=-1, keepdims=True))


def vector(ref):
    return ref[...].astype(F32).reshape(1, -1)


def layer_kernel(n_dev, attn_scale,
                 x, dy, g1, s1, bo, g2, s2, bd, wqkv, bqkv, wo, wu, bu, wd,
                 y_out, dx_out, vec_out, dwqkv_out, dwo_out, dwu_out, dbu_out, dwd_out,
                 h1own, h1, wob, wp, wqp, wq, q_s, k_s, v_s, qkvt, big, lse, o_own, o_all, wo_all, x1, hh, dyy, ga, dza, acc, dx1,
                 do_send, do_all, do_s, delta, dqt, p_b, ds_b, dqkvt, wq_cat, dh_send, dh_pair, dh_all, dwq, dwq_r,
                 dwp, prx, frx, dwop, dwo_pr, dwo_rx, vec, vec_all,
                 hs_ss, hs_rs, hp_ss, hp_rs, wq_ss, wq_rs, wb_ss, wb_rs, o_ss, o_rs, do_ss, do_rs, dhp_ss, dhp_rs, dh_ss, dh_rs,
                 wp_ss, wp_rs, mt_ss, mt_rs, pr_ss, pr_rs, fr_ss, fr_rs, op_ss, op_rs, ox_ss, ox_rs, v_ss, v_rs):
    me = lax.axis_index("tp")
    chips = n_dev // 2
    chip, core = lax.div(me, 2), lax.rem(me, 2)
    seq = lax.div(chip, chips // 2)
    mate = 2 * (chips - 1 - chip) + core
    side = chip + 1 - 2 * lax.rem(chip, 2)
    flank, across = 2 * side + core, 2 * (chips - 1 - side) + core

    def dev(shift, other):
        return 2 * lax.rem(chip + shift + chips, chips) + (1 - core if other else core)

    PT = dev(0, True)

    def handler(n, st):
        return n if (n // 2) // (chips // 2) == st else 2 * (chips - 1 - n // 2) + n % 2

    def rc(src, dst, ssem, rsem, target):
        return pltpu.make_async_remote_copy(src_ref=src, dst_ref=dst, send_sem=ssem, recv_sem=rsem,
                                            device_id={"tp": target}, device_id_type=MESH)

    def m256(i):
        return pl.ds(i * TOK, TOK) if isinstance(i, int) else pl.ds(pl.multiple_of(i * TOK, TOK), TOK)

    def m64(i):
        return pl.ds(i * HEAD, HEAD) if isinstance(i, int) else pl.ds(pl.multiple_of(i * HEAD, HEAD), HEAD)
    barrier = pltpu.get_barrier_semaphore()
    for i in range(n_dev):
        @pl.when(me != i)
        def _():
            pl.semaphore_signal(barrier, inc=1, device_id={"tp": i}, device_id_type=MESH)

    gain1, shift1 = vector(g1), vector(s1)
    for b in range(2):
        for r in range(2):
            rows = slice(b * TOK + r * HALF, b * TOK + r * HALF + HALF)
            x_hat, _ = norm_stats(x[rows, :].astype(F32))
            h1own[b, r * HALF:r * HALF + HALF, :] = (x_hat * gain1 + shift1).astype(BF16)
    h1[m256(me), :] = h1own[seq]
    wqp[0, 0:QKV, :] = wqkv[...]
    bq_row = jnp.concatenate([bqkv[c].astype(F32) for c in range(THREE)] + [jnp.zeros((1, TAIL), F32)], axis=1)
    wqp[0, QKV:WQ_ROWS, :] = jnp.broadcast_to(bq_row, (PACK, WIDTH)).astype(BF16)

    def h1_copy(step):
        src, row, target = ((h1own.at[1 - seq], me, mate), (h1own.at[seq], me, flank), (h1.at[m256(mate), :], mate, flank))[step]
        return rc(src, h1.at[m256(row), :], hs_ss.at[step], hs_rs.at[step], target)

    def h1_recv(step, src):
        return rc(h1own.at[0], h1.at[m256(2 * src + core), :], hs_ss.at[0], hs_rs.at[step], PT)

    def h1_pair(src, received):
        rows = m256(2 * src + (1 - core if received else core))
        return rc(h1.at[rows, :], h1.at[rows, :], hp_ss.at[src], hp_rs.at[src], PT)

    def wq_copy():
        return rc(wqp.at[0], wqp.at[1], wq_ss.at[0], wq_rs.at[0], mate)
    pl.semaphore_wait(barrier, n_dev - 1)
    h1_copy(0).start()
    h1_copy(1).start()
    h1_pair(chip, False).start()
    wob[me, 0:HEAD, :] = wo[...]
    wob[me, HEAD:80, 0:TOK] = jnp.broadcast_to(vector(bu), (PACK, TOK)).astype(BF16)
    wob[me, HEAD:80, TOK:WIDTH] = jnp.zeros((PACK, TOK), BF16)
    wp[me, 0:TOK, :] = wd[...]
    wp[me, TOK:WIDTH, :] = wu[...].astype(F32).T.astype(BF16)
    dyy[0:WIDTH, :] = dy[...]

    def twin(d):
        return d + 1 - 2 * core

    w_plan = ((me, PT, PT, 0, WIDTH), (me, mate, mate, 0, TOK), (me, mate, mate, TOK, TOK), (me, flank, flank, 0, WIDTH),
              (mate, flank, across, 0, TOK), (mate, flank, across, TOK, TOK),
              (flank, PT, twin(flank), 0, WIDTH), (mate, PT, twin(mate), 0, WIDTH), (across, PT, twin(across), 0, WIDTH))

    def w_copy(step, received=False):
        own, target, got, off, size = w_plan[step]
        v = wp.at[got if received else own, pl.ds(off, size), :]
        return rc(v, v, wp_ss.at[step], wp_rs.at[step], target)

    def w_wait(*steps):
        for step in steps:
            w_copy(step, True).wait_recv()

    def w_start(*steps):
        for step in steps:
            w_copy(step).start()

    o_plan = ((me, PT, PT), (me, mate, mate), (me, flank, flank), (mate, flank, across),
              (flank, PT, twin(flank)), (mate, PT, twin(mate)), (across, PT, twin(across)))

    def wo_all_copy(step, received=False):
        own, target, got = o_plan[step]
        v = wob.at[got if received else own]
        return rc(v, v, wb_ss.at[step], wb_rs.at[step], target)

    def wo_wait(*steps):
        for step in steps:
            wo_all_copy(step, True).wait_recv()

    def wo_start(*steps):
        for step in steps:
            wo_all_copy(step).start()

    wo_start(0)

    def mate_copy(step):
        src, dst = ((hh.at[0:TOK], hh.at[WIDTH:768]), (hh.at[TOK:WIDTH], hh.at[768:1024]), (dyy.at[0:WIDTH], dyy.at[WIDTH:1024]))[step]
        return rc(src, dst, mt_ss.at[step], mt_rs.at[step], mate)

    w_start(0)

    def natural(hi):
        full = jnp.concatenate([wqp[hi, 0:QKV, :].astype(F32), jnp.zeros((HEAD, WIDTH), F32)], axis=0)
        wq[:, hi * TOK:(hi + 1) * TOK] = full.T.astype(BF16)

    natural(0)

    def project(owner, hi):
        rows = m256(owner)
        bias = wqp[hi, QKV:WQ_ROWS, 0:TOK].astype(F32)[0:1, :]
        part = (mm(h1[rows, :], wq[:, hi * TOK:(hi + 1) * TOK]) + bias).astype(BF16).astype(F32)
        q_s[hi, rows, :] = part[:, 0:HEAD].astype(BF16)
        k_s[hi, rows, :] = part[:, HEAD:HALF].astype(BF16)
        v_s[hi, rows, :] = part[:, HALF:QKV].astype(BF16)
        qkvt[hi, :, rows] = part.T[:QKV, :].astype(BF16)

    def near(t):
        base = chip + lax.div(t, 2) * (side - chip)
        return base + lax.rem(t, 2) * (chips - 1 - 2 * base)
    @pl.loop(0, chips)
    def _(t):
        src = near(t)

        @pl.when(t == 2)
        def _():
            wq_copy().start()
            wo_start(1, 2)
            w_start(1, 2, THREE)

        @pl.when(t > 0)
        def _():
            h1_recv(t - 1, src).wait_recv()
            h1_pair(src, False).start()

        @pl.when(t == 1)
        def _():
            h1_copy(2).start()

        project(2 * src + core, 0)
        h1_pair(src, True).wait_recv()
        project(2 * src + 1 - core, 0)


    s_fac = attn_scale * LOG2E
    keep = lax.broadcasted_iota(jnp.int32, (TOK, TOK), 0) <= lax.broadcasted_iota(jnp.int32, (TOK, TOK), 1)

    def o_copy(hi, j):
        head = me + hi * (mate - me)
        return rc(o_own.at[hi, :, m256(j)], o_all.at[m64(head), m256(seq)], o_ss.at[hi, j], o_rs.at[seq, head], j)

    def fold(value, op):
        return op(value.reshape(32, SUB, TOK), axis=0)

    def attend(hi, j):
        cols = m256(j)
        q_t = qkvt[hi, 0:HEAD, cols]
        base = SUB * (j % 2)
        m = jnp.full((SUB, TOK), -1e30, F32)
        for kc in range(j + 1):
            s = mm(k_s[hi, m256(kc), :], q_t) * s_fac
            if kc == j:
                s = jnp.where(keep, s, -1e30)
            big[base + kc] = s
            m = jnp.maximum(m, fold(s, jnp.max))
        m = jnp.max(m, axis=0, keepdims=True)
        l = jnp.zeros((SUB, TOK), F32)
        for kc in range(j + 1):
            l = l + fold(jnp.exp2(big[base + kc] - m), jnp.sum)
        lse_j = m + jnp.log2(jnp.sum(l, axis=0, keepdims=True))
        lse[hi, :, cols] = lse_j
        o = jnp.zeros((HEAD, TOK), F32)
        for kc in range(j + 1):
            p = jnp.exp2(big[base + kc] - lse_j).astype(BF16)
            o = o + mm(qkvt[hi, HALF:QKV, m256(kc)], p)
        o = o.astype(BF16)
        o_own[hi, :, cols] = o

        @pl.when(me != j)
        def _():
            o_copy(hi, j).start()

        @pl.when(me == j)
        def _():
            o_all[m64(me + hi * (mate - me)), m256(seq)] = o
    @pl.loop(0, 2)
    def _(hi):
        @pl.when(hi == 1)
        def _():
            wq_copy().wait_recv()
            natural(1)

            @pl.loop(0, n_dev)
            def _(owner):
                project(owner, 1)

        for j in range(n_dev):
            attend(hi, j)
            if j == 2:
                @pl.when(hi == 1)
                def _():
                    wo_wait(1)
                    wo_start(THREE, 5)
            if j == 6:
                @pl.when(hi == 1)
                def _():
                    wo_wait(2, THREE)
                    wo_start(FOUR, 6)
    mate_copy(2).start()
    w_wait(1, 2)
    w_start(FOUR, 5)
    w_wait(THREE)
    w_start(6, 7)
    wo_wait(0, FOUR, 5, 6)
    for n in range(n_dev):
        wo_all[n * HEAD:(n + 1) * HEAD, :] = wob[n, 0:HEAD, :]
    for st in range(2):
        for n in range(n_dev):
            @pl.when(me != handler(n, st))
            def _():
                rc(o_own.at[0, :, m256(0)], o_all.at[m64(n), m256(st)], o_ss.at[0, 0], o_rs.at[st, n], PT).wait_recv()

    bias_o = vector(bo)
    gain2, shift2 = vector(g2), vector(s2)
    for r in range(FOUR):
        rows = slice(r * HALF, r * HALF + HALF)
        attn = mm(o_all[:, rows], wo_all[...], 0, 0)
        x1_r = (x[rows, :].astype(F32) + attn + bias_o).astype(BF16)
        x1[rows, :] = x1_r
        x_hat, _ = norm_stats(x1_r.astype(F32))
        hh[rows, :] = (x_hat * gain2 + shift2).astype(BF16)
        if r % 2 == 1:
            mate_copy(r // 2).start()

    def mlp(n, rows):
        w2 = wp[n, 0:TOK, :]
        w1t = wp[n, TOK:WIDTH, :]
        bias_u = wob[n, HEAD:80, 0:TOK].astype(F32)[0:1, :]
        z = (mm(hh[rows, :], w1t, 1, 1) + bias_u).astype(BF16).astype(F32)
        z2 = z * z
        h = 0.5 * jnp.tanh(z * (GELU_A + GELU_AB * z2)) + 0.5
        g = z * h
        slope = h + g * ((1.0 - h) * (2.0 * GELU_A + 6.0 * GELU_AB * z2))
        dgl = mm(dyy[rows, :], w2, 1, 1).astype(BF16).astype(F32)
        dz = (dgl * slope).astype(BF16)
        ga[n, rows, :] = g.astype(BF16)
        dza[n, rows, :] = dz
        return dz, w1t
    acc[...] = jnp.zeros_like(acc)

    @pl.loop(0, n_dev)
    def _(i):
        t, other = lax.div(i, 2), lax.rem(i, 2)
        near_chip = chip + lax.rem(t, 2) * (side - chip)
        n = 2 * (near_chip + lax.div(t, 2) * (chips - 1 - 2 * near_chip)) + core + other * (1 - 2 * core)
        for step, at in ((0, 1), (6, THREE), (7, 5), (SUB, 7)):
            @pl.when(i == at)
            def _():
                w_wait(step)

        @pl.when(i == 6)
        def _():
            w_wait(FOUR, 5)
            w_start(SUB)

        for r in range(2):
            rows = slice(r * TOK, r * TOK + TOK)
            dz, w1t = mlp(n, rows)
            acc[rows, :] += mm(dz, w1t)
    vec[...] = jnp.zeros_like(vec)
    for r in range(FOUR):
        rows = slice(r * HALF, r * HALF + HALF)
        dh2 = acc[rows, :].astype(BF16).astype(F32)
        x_hat, inv_std = norm_stats(x1[rows, :].astype(F32))
        dy_r = dy[rows, :].astype(F32)
        dx1_r = (dy_r + norm_back(dh2, x_hat, inv_std, gain2)).astype(BF16)
        dx1[rows, :] = dx1_r
        vec[2:THREE, :] += jnp.sum(dx1_r.astype(F32), axis=0, keepdims=True)
        vec[THREE:FOUR, :] += jnp.sum(dh2 * x_hat, axis=0, keepdims=True)
        vec[FOUR:5, :] += jnp.sum(dh2, axis=0, keepdims=True)
        vec[5:6, :] += jnp.sum(dy_r, axis=0, keepdims=True)

    def do_copy(n, st):
        target = handler(n, st)
        hi = 0 if target == n else 1
        return rc(do_send.at[m64(n), m256(st)], do_all.at[hi, :, m256(me)], do_ss.at[n, st], do_rs.at[hi, me], target)

    for r in range(2):
        rows = slice(r * TOK, r * TOK + TOK)
        do_send[rows, :] = mm(wo_all[rows, :], dx1[...], 1, 1).astype(BF16)
    for n in range(n_dev):
        for st in range(2):
            @pl.when(me != handler(n, st))
            def _():
                do_copy(n, st).start()

            @pl.when(me == handler(n, st))
            def _():
                do_all[0 if handler(n, st) == n else 1, :, m256(me)] = do_send[m64(n), m256(st)]

    def wo_pair_copy(slot):
        return rc(dwop.at[2 * slot + 1 - core], dwo_pr.at[slot], op_ss.at[slot], op_rs.at[slot], PT)

    def wo_copy(t):
        return rc(dwop.at[2 * t + core], dwo_rx.at[chip], ox_ss.at[t], ox_rs.at[chip], 2 * t + core)
    for n in range(n_dev):
        dwop[n] = mm(o_all[m64(n), :], dx1[...])
    for t in range(chips):
        wo_pair_copy(t).start()

    def pair_copy(which):
        return rc(dwp.at[2 * which], prx.at[which], pr_ss.at[which], pr_rs.at[which], PT)

    def side_copy(step):
        rows = pl.ds(step * (G_ROWS // THREE), G_ROWS // THREE)
        return rc(dwp.at[1, rows], frx.at[rows], fr_ss.at[step], fr_rs.at[step], flank)

    def pair_add(which):
        pair_copy(which).wait_recv()
        dwp[2 * which + 1] += prx[which]

    for t in range(chips):
        wo_pair_copy(t).wait_recv()
        dwop[2 * t + core] += dwo_pr[t]

    wo_copy(side).start()

    def block(i):
        which, own = lax.div(i, 2), lax.rem(i, 2)
        return which, own, 2 * (side + which * (chip - side)) + (1 - core) + own * (2 * core - 1)
    @pl.loop(0, FOUR)
    def _(i):
        _, _, n = block(i)
        own_rows = slice(0, WIDTH)
        dwp[i, 0:TOK, :] = mm(ga[n, own_rows, :], dyy[own_rows, :], 0, 0)
        dwp[i, TOK:WIDTH, :] = mm(dza[n, own_rows, :], hh[own_rows, :], 0, 0)
        dwp[i, WIDTH:528, 0:TOK] = jnp.broadcast_to(jnp.sum(dza[n, own_rows, :].astype(F32), axis=0, keepdims=True), (PACK, TOK))
        dwp[i, WIDTH:528, TOK:WIDTH] = jnp.zeros((PACK, TOK), F32)
    mate_copy(2).wait_recv()
    for r in range(2):
        mate_copy(r).wait_recv()
        rows = slice(WIDTH + r * TOK, 768 + r * TOK)
        @pl.loop(0, FOUR)
        def _(i):
            which, own, n = block(i)
            mlp(n, rows)
            dwp[i, 0:TOK, :] += mm(ga[n, rows, :], dyy[rows, :], 0, 0)
            dwp[i, TOK:WIDTH, :] += mm(dza[n, rows, :], hh[rows, :], 0, 0)
            dwp[i, WIDTH:528, 0:TOK] += jnp.broadcast_to(jnp.sum(dza[n, rows, :].astype(F32), axis=0, keepdims=True), (PACK, TOK))
            if r == 1:
                @pl.when(own == 0)
                def _():
                    pair_copy(which).start()

                @pl.when(i == 2)
                def _():
                    pair_add(0)
                    for step in range(THREE):
                        side_copy(step).start()

    pair_add(1)

    for j in range(n_dev):
        for hi in range(2):
            @pl.when(me != j)
            def _():
                rc(do_send.at[m64(0), m256(0)], do_all.at[hi, :, m256(j)], do_ss.at[0, 0], do_rs.at[hi, j], PT).wait_recv()
            do_t = do_all[hi, :, m256(j)].astype(F32)
            do_s[hi, m256(j), :] = do_t.T.astype(BF16)
            delta[hi, :, m256(j)] = jnp.sum(do_t * o_own[hi, :, m256(j)].astype(F32), axis=0, keepdims=True)
    for t in range(chips):
        @pl.when((chip != t) & (side != t))
        def _():
            wo_copy(t).start()
    dwq[...] = jnp.zeros_like(dwq)
    for hi in range(2):
        wq_cat[hi * QKV:(hi + 1) * QKV, :] = wqp[hi, 0:QKV, :]

    def dwq_copy():
        return rc(dwq.at[1], dwq_r, wq_ss.at[1], wq_rs.at[1], mate)

    def dh_pair_copy(kb):
        return rc(dh_send.at[kb], dh_pair.at[kb // 2], dhp_ss.at[kb // 2], dhp_rs.at[kb // 2], PT)

    def dh_copy(kb):
        return rc(dh_send.at[kb], dh_all.at[chip], dh_ss.at[kb // 2], dh_rs.at[chip], kb)

    def dh_finish(kb):
        @pl.when(core == kb % 2)
        def _():
            dh_pair_copy(kb).wait_recv()
            total = (dh_send[kb].astype(F32) + dh_pair[kb // 2].astype(F32)).astype(BF16)
            dh_send[kb] = total

            @pl.when(me != kb)
            def _():
                dh_copy(kb).start()

            @pl.when(me == kb)
            def _():
                dh_all[chip] = total
    @pl.loop(0, 2)
    def _(i):
        hi = 1 - i
        base = pl.multiple_of(QKV * hi, HEAD)

        @pl.when(i == 1)
        def _():
            dwq_copy().start()

        for kb in range(n_dev):
            rows = m256(kb)
            late = slice(kb * TOK, n_dev * TOK)
            for qb in range(kb, n_dev):
                cols = m256(qb)
                for c in range(2):
                    part = slice(c * HALF, c * HALF + HALF)
                    keys = slice(kb * TOK + c * HALF, kb * TOK + c * HALF + HALF)
                    p = jnp.exp2(mm(k_s[hi, keys, :], qkvt[hi, 0:HEAD, cols]) * s_fac - lse[hi, :, cols])
                    if qb == kb:
                        p = jnp.where(keep[part], p, 0.0)
                    dp = mm(v_s[hi, keys, :], do_all[hi, :, cols]).astype(BF16).astype(F32)
                    p_b[kb % 2, part, cols] = p.astype(BF16)
                    ds_b[kb % 2, part, cols] = (p * (dp - delta[hi, :, cols])).astype(BF16)
            dv = mm(p_b[kb % 2, :, late], do_s[hi, late, :])
            dk = mm(ds_b[kb % 2, :, late], q_s[hi, late, :]) * attn_scale
            dq = mm(qkvt[hi, HEAD:HALF, rows], ds_b[kb % 2, :, late])
            if kb == 0:
                dqt[...] = dq
            else:
                dqt[:, late] += dq
            dqkvt[pl.ds(base, HEAD), rows] = (dqt[:, rows] * attn_scale).astype(BF16)
            dqkvt[pl.ds(base + HEAD, HALF), rows] = jnp.concatenate([dk, dv], axis=1).T.astype(BF16)

            @pl.when(i == 1)
            def _():
                dh = mm(dqkvt[:, rows], wq_cat[...], 0, 0)
                dh_send[kb] = dh.astype(BF16)

                @pl.when(core != kb % 2)
                def _():
                    dh_pair_copy(kb).start()

                if kb > 0:
                    dh_finish(kb - 1)


        mine = dqkvt[pl.ds(base, QKV), :]
        dwq[hi, 0:QKV, :] = mm(mine, h1[...])
        dwq[hi, QKV:DW_ROWS, 0:QKV] = mm(jnp.ones((SUB, SEQ), BF16), mine, 1, 1)

    dh_finish(n_dev - 1)

    for step in range(THREE):
        side_copy(step).wait_recv()
    dwd_out[...] = dwp[THREE, 0:TOK, :] + frx[0:TOK, :]
    dwu_out[...] = (dwp[THREE, TOK:WIDTH, :] + frx[TOK:WIDTH, :]).T
    dbu_out[...] = dwp[THREE, WIDTH:520, 0:TOK] + frx[WIDTH:520, 0:TOK]
    dwo_rx[chip] = dwop[me]
    for t in range(chips):
        @pl.when(chip != t)
        def _():
            rc(dwop.at[0], dwo_rx.at[t], ox_ss.at[0], ox_rs.at[t], PT).wait_recv()
    dwo_out[...] = dwo_rx[0] + dwo_rx[1] + dwo_rx[2] + dwo_rx[THREE]

    acc[...] = jnp.zeros_like(acc)

    @pl.loop(0, n_dev)
    def _(n):
        for r in range(2):
            rows = slice(r * TOK, r * TOK + TOK)
            acc[rows, :] += mm(ga[n, rows, :], wp[n, 0:TOK, :])

    y_out[...] = (x1[...].astype(F32) + acc[...] + vector(bd)).astype(BF16)

    for t in range(chips):
        @pl.when(chip != t)
        def _():
            rc(dh_send.at[0], dh_all.at[t], dh_ss.at[0], dh_rs.at[t], PT).wait_recv()
    for r in range(FOUR):
        rows = slice(r * HALF, r * HALF + HALF)
        half = slice((r % 2) * HALF, (r % 2) * HALF + HALF)
        first = (r // 2) * (chips // 2)
        dh1 = (dh_all[first, half, :].astype(F32) + dh_all[first + 1, half, :].astype(F32)).astype(BF16).astype(F32)
        x_hat, inv_std = norm_stats(x[rows, :].astype(F32))
        dx_out[rows, :] = (dx1[rows, :].astype(F32) + norm_back(dh1, x_hat, inv_std, gain1)).astype(BF16)
        vec[0:1, :] += jnp.sum(dh1 * x_hat, axis=0, keepdims=True)
        vec[1:2, :] += jnp.sum(dh1, axis=0, keepdims=True)

    def vec_copy(j):
        return rc(vec, vec_all.at[me], v_ss.at[j], v_rs.at[me], j)
    for j in range(n_dev):
        @pl.when(me != j)
        def _():
            vec_copy(j).start()
    vec_all[me] = vec[...]
    dwq_copy().wait_recv()
    dwqkv_out[...] = dwq[0] + dwq_r[...]
    for j in range(n_dev):
        @pl.when(me != j)
        def _():
            rc(vec, vec_all.at[j], v_ss.at[0], v_rs.at[j], PT).wait_recv()
    total = vec_all[0]
    for j in range(1, n_dev):
        total = total + vec_all[j]
    vec_out[...] = total

    wq_copy().wait_send()
    dwq_copy().wait_send()
    for t in range(chips):
        h1_pair(t, False).wait_send()

        @pl.when(chip != t)
        def _():
            wo_copy(t).wait_send()

        wo_pair_copy(t).wait_send()
    for step in range(9):
        w_copy(step).wait_send()
    for step in range(7):
        wo_all_copy(step).wait_send()
    for step in range(THREE):
        h1_copy(step).wait_send()
    for step in range(THREE):
        mate_copy(step).wait_send()
    for which in range(2):
        pair_copy(which).wait_send()
    for step in range(THREE):
        side_copy(step).wait_send()
    for j in range(n_dev):
        @pl.when(me != j)
        def _():
            vec_copy(j).wait_send()
            for hi in range(2):
                o_copy(hi, j).wait_send()

        for st in range(2):
            @pl.when(me != handler(j, st))
            def _():
                do_copy(j, st).wait_send()

        @pl.when(core != j % 2)
        def _():
            dh_pair_copy(j).wait_send()

        @pl.when((core == j % 2) & (me != j))
        def _():
            dh_copy(j).wait_send()


def finish_kernel(y, dx, vec, dwqkv, dwo, dwu, dbu, dwd, y_o, dx_o, v0, v1, dwqkv_o, dbqkv_o, dwo_o, v2, v3, v4, dwu_o, dbu_o, dwd_o, v5):
    y_o[...] = y[...]
    dx_o[...] = dx[...]
    for i, ref in enumerate((v0, v1, v2, v3, v4, v5)):
        ref[...] = vec[i:i + 1, :].reshape(ref.shape)
    dwqkv_o[...] = dwqkv[0:QKV, :]
    for c in range(THREE):
        dbqkv_o[c] = dwqkv[QKV:193, c * HEAD:(c + 1) * HEAD]
    dwo_o[...] = dwo[...]
    dwu_o[...] = dwu[...]
    dbu_o[...] = dbu[0:1, :].reshape(dbu_o.shape)
    dwd_o[...] = dwd[...]


def solution(mesh):
    n_dev = mesh.shape["tp"]

    def device_step(hidden, grad_out, ln1_gain, ln1_bias, w_qkv, b_qkv, w_out, b_out, ln2_gain, ln2_bias, w_up, b_up, w_down, b_down):
        batch, tokens, d = hidden.shape
        rows = batch * tokens
        head = w_qkv.shape[-1]
        seq = tokens * n_dev
        ff = w_up.shape[1]
        chips = n_dev // 2
        attn_scale = head ** -0.5
        sds = jax.ShapeDtypeStruct
        vm = pltpu.VMEM

        def dma(*shape):
            return pltpu.SemaphoreType.DMA(shape)

        vspec = pl.BlockSpec(memory_space=pltpu.VMEM)
        outs = pl.pallas_call(
            lambda *refs: layer_kernel(n_dev, attn_scale, *refs),
            out_shape=(sds((rows, d), BF16), sds((rows, d), BF16), sds((SUB, d), F32), sds((DW_ROWS, d), F32),
                       sds((head, d), F32), sds((d, ff), F32), sds((SUB, ff), F32), sds((ff, d), F32)),
            in_specs=[vspec] * 14,
            out_specs=tuple([vspec] * SUB),
            scratch_shapes=[
                vm((2, tokens, d), BF16), vm((seq, d), BF16), vm((n_dev, WO_ROWS, d), BF16), vm((n_dev, 2 * ff, d), BF16),
                vm((2, WQ_ROWS, d), BF16), vm((d, WIDTH), BF16),
                vm((2, seq, head), BF16), vm((2, seq, head), BF16), vm((2, seq, head), BF16), vm((2, THREE * head, seq), BF16),
                vm((PACK, TOK, TOK), F32), vm((2, 1, seq), F32), vm((2, head, seq), BF16), vm((n_dev * head, rows), BF16),
                vm((n_dev * head, d), BF16), vm((rows, d), BF16), vm((2 * rows, d), BF16), vm((2 * rows, d), BF16),
                vm((n_dev, 2 * rows, ff), BF16), vm((n_dev, 2 * rows, ff), BF16), vm((rows, d), F32), vm((rows, d), BF16),
                vm((n_dev * head, rows), BF16), vm((2, head, seq), BF16), vm((2, seq, head), BF16),
                vm((2, 1, seq), F32), vm((head, seq), F32), vm((2, TOK, seq), BF16), vm((2, TOK, seq), BF16), vm((6 * head, seq), BF16), vm((6 * head, d), BF16),
                vm((n_dev, tokens, d), BF16), vm((chips, tokens, d), BF16), vm((chips, tokens, d), BF16),
                vm((2, DW_ROWS, d), F32), vm((DW_ROWS, d), F32),
                vm((FOUR, G_ROWS, d), F32), vm((2, G_ROWS, d), F32), vm((G_ROWS, d), F32),
                vm((n_dev, head, d), F32), vm((chips, head, d), F32), vm((chips, head, d), F32),
                vm((SUB, d), F32), vm((n_dev, SUB, d), F32),
                dma(chips), dma(chips), dma(chips), dma(chips), dma(2), dma(2), dma(7), dma(7), dma(2, n_dev), dma(2, n_dev),
                dma(n_dev, 2), dma(2, n_dev), dma(chips), dma(chips), dma(chips), dma(chips),
                dma(9), dma(9), dma(THREE), dma(THREE), dma(2), dma(2), dma(THREE), dma(THREE), dma(chips), dma(chips), dma(chips), dma(chips), dma(n_dev), dma(n_dev),
            ],
            compiler_params=pltpu.CompilerParams(collective_id=0, has_side_effects=True, vmem_limit_bytes=67043328),
            name="layer",
        )(hidden.reshape(rows, d), grad_out.reshape(rows, d), ln1_gain, ln1_bias, b_out, ln2_gain, ln2_bias, b_down,
          w_qkv.transpose(1, 2, THREE, 0).reshape(THREE * head, d), b_qkv, w_out.reshape(head, d), w_up, b_up, w_down)
        v1d = sds((d,), F32)
        y, dx, v0, v1, dwqkv_t, dbqkv, dwo, v2, v3, v4, dwu, dbu, dwd, v5 = pl.pallas_call(
            finish_kernel,
            out_shape=(sds((rows, d), BF16), sds((rows, d), BF16), v1d, v1d, sds((THREE * head, d), F32), sds((THREE, 1, head), F32),
                       sds((head, d), F32), v1d, v1d, v1d, sds((d, ff), F32), sds((ff,), F32), sds((ff, d), F32), v1d),
            in_specs=[vspec] * SUB,
            out_specs=tuple([vspec] * 14),
            name="finish",
        )(*outs)
        return (y.reshape(hidden.shape), dx.reshape(hidden.shape), v0, v1, dwqkv_t.reshape(THREE, 1, head, d).transpose(THREE, 0, 1, 2),
                dbqkv, dwo.reshape(w_out.shape), v2, v3, v4, dwu, dbu, dwd, v5)

    act_spec = P("dp", "tp", None)
    vec_spec = P(None)
    group_vec = P("dp")
    in_specs = (act_spec, act_spec, vec_spec, vec_spec, P(None, None, "tp", None), P(None, "tp", None), P("tp", None, None), vec_spec, vec_spec, vec_spec, P(None, "tp"), P("tp"), P("tp", None), vec_spec)
    out_specs = (act_spec, act_spec, group_vec, group_vec, P("dp", None, "tp", None), P("dp", "tp", None), P(("dp", "tp"), None, None), group_vec, group_vec, group_vec, P("dp", "tp"), P(("dp", "tp")), P(("dp", "tp"), None), group_vec)
    return jax.shard_map(device_step, mesh=mesh, in_specs=in_specs, out_specs=out_specs, check_vma=False)
```

time: 129 us -> 126 us (0.977)
  Pallas kernels: 126 us -> 123 us
    pallas_call x1, Pallas kernels: 123 us -> 120 us  [device_step(): pl.pallas_call(lambda *refs: layer_kernel(n_dev, attn_scale, *refs), out_...]
where the time goes in v4:
time: 126 us; the launch traced here: 125 us
  Pallas kernels  123 us (98%)
    pallas_call x1, Pallas kernels, device_step(): pl.pallas_call(lambda *refs: layer_kernel(n_dev, attn_scale, *refs), out_...  120 us
    pallas_call x1, Pallas kernels, device_step(): pl.pallas_call(finish_kernel, out_shape=(sds((rows, d), BF16), sds((rows,...  3.3 us

profile of v4, /device:TPU:113, one launch (start us, length us, event | category | flops | bytes accessed | tf_op | source)
XLA Modules:
  0.0 125.5 jit_solution(7042888158914374488)
XLA Ops:
  0.6 0.0 copy-start
  0.7 0.7 copy-done
  1.3 0.6 copy.28.refs_9_
  1.9 120.1 %layer.1 = (bf16[512,512]{1,0:T(8,128)(2,1)}, bf16[512,512]{1,0:T(8,128)(2,1)}, f32[8,512]{1,0:T(8,128)}, f32[200,512]{1,0:T(8,128)}, f32[64,512]{1,0:T(8,128)},...) custom-call(bf16[512,512]{1,0:T(8,128)(2,1)} %bitcast.14, bf16[512,512]{1,0:T(8,128)(2,1)} %bitcast.15, ...), custom_call_target="tpu_custom_call" | custom-call | tf_op jit(solution)/shard_map/layer/pallas_call | solution.py:650
  122.0 3.3 %finish.1 = (bf16[512,512]{1,0:T(8,128)(2,1)}, bf16[512,512]{1,0:T(8,128)(2,1)}, f32[512]{0:T(512)}, f32[512]{0:T(512)}, f32[192,512]{1,0:T(8,128)}, /*index=5*/...) custom-call(bf16[512,512]{1,0:T(8,128)(2,1)} %get-tuple-element.36.y, ...), custom_call_target="tpu_custom_call" | custom-call | tf_op jit(solution)/shard_map/finish/pallas_call | solution.py:679
Async XLA Ops:
  0.6 0.7 copy-start

commit v5 on v4

--- a/solution.py
+++ b/solution.py
@@ -313,6 +313,20 @@
         ga[n, rows, :] = g.astype(BF16)
         dza[n, rows, :] = dz
         return dz, w1t
+
+    def block(i):
+        which, own = lax.div(i, 2), lax.rem(i, 2)
+        return which, own, 2 * (side + which * (chip - side)) + (1 - core) + own * (2 * core - 1)
+
+    def own_grads():
+        @pl.loop(0, FOUR)
+        def _(i):
+            _, _, n = block(i)
+            own_rows = slice(0, WIDTH)
+            dwp[i, 0:TOK, :] = mm(ga[n, own_rows, :], dyy[own_rows, :], 0, 0)
+            dwp[i, TOK:WIDTH, :] = mm(dza[n, own_rows, :], hh[own_rows, :], 0, 0)
+            dwp[i, WIDTH:528, 0:TOK] = jnp.broadcast_to(jnp.sum(dza[n, own_rows, :].astype(F32), axis=0, keepdims=True), (PACK, TOK))
+            dwp[i, WIDTH:528, TOK:WIDTH] = jnp.zeros((PACK, TOK), F32)
     acc[...] = jnp.zeros_like(acc)
 
     @pl.loop(0, n_dev)
@@ -327,6 +341,7 @@
 
         @pl.when(i == 6)
         def _():
+            own_grads()
             w_wait(FOUR, 5)
             w_start(SUB)
 
@@ -355,16 +370,6 @@
     for r in range(2):
         rows = slice(r * TOK, r * TOK + TOK)
         do_send[rows, :] = mm(wo_all[rows, :], dx1[...], 1, 1).astype(BF16)
-    for n in range(n_dev):
-        for st in range(2):
-            @pl.when(me != handler(n, st))
-            def _():
-                do_copy(n, st).start()
-
-            @pl.when(me == handler(n, st))
-            def _():
-                do_all[0 if handler(n, st) == n else 1, :, m256(me)] = do_send[m64(n), m256(st)]
-
     def wo_pair_copy(slot):
         return rc(dwop.at[2 * slot + 1 - core], dwo_pr.at[slot], op_ss.at[slot], op_rs.at[slot], PT)
 
@@ -391,22 +396,20 @@
         dwop[2 * t + core] += dwo_pr[t]
 
     wo_copy(side).start()
-
-    def block(i):
-        which, own = lax.div(i, 2), lax.rem(i, 2)
-        return which, own, 2 * (side + which * (chip - side)) + (1 - core) + own * (2 * core - 1)
-    @pl.loop(0, FOUR)
-    def _(i):
-        _, _, n = block(i)
-        own_rows = slice(0, WIDTH)
-        dwp[i, 0:TOK, :] = mm(ga[n, own_rows, :], dyy[own_rows, :], 0, 0)
-        dwp[i, TOK:WIDTH, :] = mm(dza[n, own_rows, :], hh[own_rows, :], 0, 0)
-        dwp[i, WIDTH:528, 0:TOK] = jnp.broadcast_to(jnp.sum(dza[n, own_rows, :].astype(F32), axis=0, keepdims=True), (PACK, TOK))
-        dwp[i, WIDTH:528, TOK:WIDTH] = jnp.zeros((PACK, TOK), F32)
     mate_copy(2).wait_recv()
     for r in range(2):
         mate_copy(r).wait_recv()
         rows = slice(WIDTH + r * TOK, 768 + r * TOK)
+        if r == 1:
+            for n in range(n_dev):
+                for st in range(2):
+                    @pl.when(me != handler(n, st))
+                    def _():
+                        do_copy(n, st).start()
+
+                    @pl.when(me == handler(n, st))
+                    def _():
+                        do_all[0 if handler(n, st) == n else 1, :, m256(me)] = do_send[m64(n), m256(st)]
         @pl.loop(0, FOUR)
         def _(i):
             which, own, n = block(i)
@@ -422,7 +425,7 @@
                 @pl.when(i == 2)
                 def _():
                     pair_add(0)
-                    for step in range(THREE):
+                    for step in range(2):
                         side_copy(step).start()
 
     pair_add(1)
@@ -517,18 +520,7 @@
         dwq[hi, QKV:DW_ROWS, 0:QKV] = mm(jnp.ones((SUB, SEQ), BF16), mine, 1, 1)
 
     dh_finish(n_dev - 1)
-
-    for step in range(THREE):
-        side_copy(step).wait_recv()
-    dwd_out[...] = dwp[THREE, 0:TOK, :] + frx[0:TOK, :]
-    dwu_out[...] = (dwp[THREE, TOK:WIDTH, :] + frx[TOK:WIDTH, :]).T
-    dbu_out[...] = dwp[THREE, WIDTH:520, 0:TOK] + frx[WIDTH:520, 0:TOK]
-    dwo_rx[chip] = dwop[me]
-    for t in range(chips):
-        @pl.when(chip != t)
-        def _():
-            rc(dwop.at[0], dwo_rx.at[t], ox_ss.at[0], ox_rs.at[t], PT).wait_recv()
-    dwo_out[...] = dwo_rx[0] + dwo_rx[1] + dwo_rx[2] + dwo_rx[THREE]
+    side_copy(2).start()
 
     acc[...] = jnp.zeros_like(acc)
 
@@ -561,6 +553,18 @@
         def _():
             vec_copy(j).start()
     vec_all[me] = vec[...]
+    for step in range(THREE):
+        side_copy(step).wait_recv()
+    dwd_out[...] = dwp[THREE, 0:TOK, :] + frx[0:TOK, :]
+    dwu_out[...] = (dwp[THREE, TOK:WIDTH, :] + frx[TOK:WIDTH, :]).T
+    dbu_out[...] = dwp[THREE, WIDTH:520, 0:TOK] + frx[WIDTH:520, 0:TOK]
+    dwo_rx[chip] = dwop[me]
+    for t in range(chips):
+        @pl.when(chip != t)
+        def _():
+            rc(dwop.at[0], dwo_rx.at[t], ox_ss.at[0], ox_rs.at[t], PT).wait_recv()
+    dwo_out[...] = dwo_rx[0] + dwo_rx[1] + dwo_rx[2] + dwo_rx[THREE]
+
     dwq_copy().wait_recv()
     dwqkv_out[...] = dwq[0] + dwq_r[...]
     for j in range(n_dev):

time: 126 us -> 120 us (0.952)
  Pallas kernels: 123 us -> 118 us
    pallas_call x1, Pallas kernels: 120 us -> 114 us  [device_step(): pl.pallas_call(lambda *refs: layer_kernel(n_dev, attn_scale, *refs), out_...]
where the time goes in v5:
time: 120 us
  Pallas kernels  118 us (98%)
  local copies, waits for them, and re-layouts  1.24 us (1%)
    pallas_call x1, Pallas kernels, device_step(): pl.pallas_call(lambda *refs: layer_kernel(n_dev, attn_scale, *refs), out_...  114 us
    pallas_call x1, Pallas kernels, device_step(): pl.pallas_call(finish_kernel, out_shape=(sds((rows, d), BF16), sds((rows,...  3.3 us

profile of v5, /device:TPU:113, one launch (start us, length us, event | category | flops | bytes accessed | tf_op | source)
XLA Modules:
  0.0 119.8 jit_solution(3577439346096216669)
XLA Ops:
  0.6 0.0 copy-start
  0.7 0.7 copy-done
  1.3 0.6 copy.28.refs_9_
  1.9 114.4 %layer.1 = (bf16[512,512]{1,0:T(8,128)(2,1)}, bf16[512,512]{1,0:T(8,128)(2,1)}, f32[8,512]{1,0:T(8,128)}, f32[200,512]{1,0:T(8,128)}, f32[64,512]{1,0:T(8,128)},...) custom-call(bf16[512,512]{1,0:T(8,128)(2,1)} %bitcast.14, bf16[512,512]{1,0:T(8,128)(2,1)} %bitcast.15, ...), custom_call_target="tpu_custom_call" | custom-call | tf_op jit(solution)/shard_map/layer/pallas_call | solution.py:654
  116.3 3.3 %finish.1 = (bf16[512,512]{1,0:T(8,128)(2,1)}, bf16[512,512]{1,0:T(8,128)(2,1)}, f32[512]{0:T(512)}, f32[512]{0:T(512)}, f32[192,512]{1,0:T(8,128)}, /*index=5*/...) custom-call(bf16[512,512]{1,0:T(8,128)(2,1)} %get-tuple-element.36.y, ...), custom_call_target="tpu_custom_call" | custom-call | tf_op jit(solution)/shard_map/finish/pallas_call | solution.py:683
Async XLA Ops:
  0.6 0.7 copy-start

commit v6 on v5

--- a/solution.py
+++ b/solution.py
@@ -53,7 +53,7 @@
                  x, dy, g1, s1, bo, g2, s2, bd, wqkv, bqkv, wo, wu, bu, wd,
                  y_out, dx_out, vec_out, dwqkv_out, dwo_out, dwu_out, dbu_out, dwd_out,
                  h1own, h1, wob, wp, wqp, wq, q_s, k_s, v_s, qkvt, big, lse, o_own, o_all, wo_all, x1, hh, dyy, ga, dza, acc, dx1,
-                 do_send, do_all, do_s, delta, dqt, p_b, ds_b, dqkvt, wq_cat, dh_send, dh_pair, dh_all, dwq, dwq_r,
+                 do_send, do_all, do_s, delta, dqt, p_b, ds_b, p_f, dqkvt, wq_cat, dh_send, dh_pair, dh_all, dwq, dwq_r,
                  dwp, prx, frx, dwop, dwo_pr, dwo_rx, vec, vec_all,
                  hs_ss, hs_rs, hp_ss, hp_rs, wq_ss, wq_rs, wb_ss, wb_rs, o_ss, o_rs, do_ss, do_rs, dhp_ss, dhp_rs, dh_ss, dh_rs,
                  wp_ss, wp_rs, mt_ss, mt_rs, pr_ss, pr_rs, fr_ss, fr_rs, op_ss, op_rs, ox_ss, ox_rs, v_ss, v_rs):
@@ -236,10 +236,10 @@
             l = l + fold(jnp.exp2(big[base + kc] - m), jnp.sum)
         lse_j = m + jnp.log2(jnp.sum(l, axis=0, keepdims=True))
         lse[hi, :, cols] = lse_j
-        o = jnp.zeros((HEAD, TOK), F32)
         for kc in range(j + 1):
-            p = jnp.exp2(big[base + kc] - lse_j).astype(BF16)
-            o = o + mm(qkvt[hi, HALF:QKV, m256(kc)], p)
+            p_f[j % 2, m256(kc), :] = jnp.exp2(big[base + kc] - lse_j).astype(BF16)
+        seen = slice(0, (j + 1) * TOK)
+        o = mm(qkvt[hi, HALF:QKV, seen], p_f[j % 2, seen, :])
         o = o.astype(BF16)
         o_own[hi, :, cols] = o
 
@@ -665,7 +665,7 @@
                 vm((n_dev * head, d), BF16), vm((rows, d), BF16), vm((2 * rows, d), BF16), vm((2 * rows, d), BF16),
                 vm((n_dev, 2 * rows, ff), BF16), vm((n_dev, 2 * rows, ff), BF16), vm((rows, d), F32), vm((rows, d), BF16),
                 vm((n_dev * head, rows), BF16), vm((2, head, seq), BF16), vm((2, seq, head), BF16),
-                vm((2, 1, seq), F32), vm((head, seq), F32), vm((2, TOK, seq), BF16), vm((2, TOK, seq), BF16), vm((6 * head, seq), BF16), vm((6 * head, d), BF16),
+                vm((2, 1, seq), F32), vm((head, seq), F32), vm((2, TOK, seq), BF16), vm((2, TOK, seq), BF16), vm((2, seq, TOK), BF16), vm((6 * head, seq), BF16), vm((6 * head, d), BF16),
                 vm((n_dev, tokens, d), BF16), vm((chips, tokens, d), BF16), vm((chips, tokens, d), BF16),
                 vm((2, DW_ROWS, d), F32), vm((DW_ROWS, d), F32),
                 vm((FOUR, G_ROWS, d), F32), vm((2, G_ROWS, d), F32), vm((G_ROWS, d), F32),

time: 120 us -> 121 us (level)
    pallas_call x1, Pallas kernels: 114 us -> 116 us  [device_step(): pl.pallas_call(lambda *refs: layer_kernel(n_dev, attn_scale, *refs), out_...]
where the time goes in v6:
time: 121 us
  Pallas kernels  119 us (98%)
  local copies, waits for them, and re-layouts  1.24 us (1%)
    pallas_call x1, Pallas kernels, device_step(): pl.pallas_call(lambda *refs: layer_kernel(n_dev, attn_scale, *refs), out_...  116 us
    pallas_call x1, Pallas kernels, device_step(): pl.pallas_call(finish_kernel, out_shape=(sds((rows, d), BF16), sds((rows,...  3.3 us

profile of v6, /device:TPU:113, one launch (start us, length us, event | category | flops | bytes accessed | tf_op | source)
XLA Modules:
  0.0 121.2 jit_solution(5361703646517951137)
XLA Ops:
  0.6 0.0 copy-start
  0.7 0.7 copy-done
  1.3 0.6 copy.28.refs_9_
  1.9 115.8 %layer.1 = (bf16[512,512]{1,0:T(8,128)(2,1)}, bf16[512,512]{1,0:T(8,128)(2,1)}, f32[8,512]{1,0:T(8,128)}, f32[200,512]{1,0:T(8,128)}, f32[64,512]{1,0:T(8,128)},...) custom-call(bf16[512,512]{1,0:T(8,128)(2,1)} %bitcast.14, bf16[512,512]{1,0:T(8,128)(2,1)} %bitcast.15, ...), custom_call_target="tpu_custom_call" | custom-call | tf_op jit(solution)/shard_map/layer/pallas_call | solution.py:654
  117.7 3.3 %finish.1 = (bf16[512,512]{1,0:T(8,128)(2,1)}, bf16[512,512]{1,0:T(8,128)(2,1)}, f32[512]{0:T(512)}, f32[512]{0:T(512)}, f32[192,512]{1,0:T(8,128)}, /*index=5*/...) custom-call(bf16[512,512]{1,0:T(8,128)(2,1)} %get-tuple-element.36.y, ...), custom_call_target="tpu_custom_call" | custom-call | tf_op jit(solution)/shard_map/finish/pallas_call | solution.py:683
Async XLA Ops:
  0.6 0.7 copy-start
